TPU v7x, 32 devices: a whole 2x2x4 slice. The times are simulated.
32 devices in a mesh: rep: 2 (over y), ada: 4 (over z), tp: 4 (over x, core).
Axes of the slice: x: 2, y: 2, z: 4, core: 2. Of those that a mesh axis runs over, the one named last changes fastest.
Arguments:
- hidden: bfloat16 [256, 8192], P(('rep', 'ada')), parts along dimension 0, may hold values from -6 to 6
- input_norm_gain: bfloat16 [8192], replicated, may hold values from 0.5 to 1.5
- request_adapter: int32 [256], P(('rep', 'ada')), parts along dimension 0, may hold values from 0 to 15, as said below
- cache_fill_length: int32 [256], P(('rep', 'ada')), parts along dimension 0, may hold values from 1 to 512, as said below
- query_weight: bfloat16 [8192, 8192], P('ada', 'tp'), may hold values from -0.0625 to 0.0625
- key_weight: bfloat16 [8192, 1024], P('ada', 'tp'), may hold values from -0.0625 to 0.0625
- value_weight: bfloat16 [8192, 1024], P('ada', 'tp'), may hold values from -0.0625 to 0.0625
- output_weight: bfloat16 [8192, 8192], P('tp', 'ada'), may hold values from -0.0625 to 0.0625
- down_weight_all: bfloat16 [8192, 512], P('tp', 'ada'), may hold values from -0.0625 to 0.0625
- query_up_weight: bfloat16 [256, 8192], P('ada', 'tp'), may hold values from -1.5 to 1.5
- value_up_weight: bfloat16 [256, 1024], P('ada', 'tp'), may hold values from -1.5 to 1.5
- rotated_key_cache: bfloat16 [256, 512, 1024], P(('rep', 'ada'), None, 'tp'), parts along dimension 0, may hold values from -768 to 768
- stored_value_cache: bfloat16 [256, 512, 1024], P(('rep', 'ada'), None, 'tp'), parts along dimension 0, may hold values from -6 to 6
Outputs:
- layer_out: bfloat16 [256, 8192], P(('rep', 'tp'), 'ada'), parts along dimension 0
- new_key: bfloat16 [256, 1024], P(('rep', 'ada'), 'tp'), parts along dimension 0
- new_value: bfloat16 [256, 1024], P(('rep', 'ada'), 'tp'), parts along dimension 0
There are 2 independent parts, one for each index of `rep`. A program takes and returns all parts, laid end to end along the dimension named above; an argument that names none is the same for every part. Nothing has to cross between parts.
Inputs may be any that keep to these rules, and one draw needn't show every extreme that they name: `request_adapter`: among the 32 requests of one ada index (aligned blocks), at most 16 name adapters of one group 4 * o to 4 * o + 3; in every draw one group is named by exactly 16 requests of every block. `cache_fill_length`: within each part of rep the 128 lengths sum to 32768, and some request of each part has exactly 512.
All inputs are finite; a program needn't handle non-finite values.
Results may differ from a plain program's by a relative error of at most 0.012.
The roundings to bfloat16 on the way count: a program that leaves them out, or rounds other values in their place, can miss the bound.
Values may be sent and summed in bfloat16 or wider, within the bound.
A program may use at most 64 MiB of HBM per device.

v0:
```python
import functools

import jax
import jax.numpy as jnp
from jax import lax
from jax.experimental import pallas as pl
from jax.experimental.pallas import tpu as pltpu
from jax.sharding import PartitionSpec as P

QUERY_HEAD_COUNT = 64
KEY_VALUE_HEADS = 8
HEAD_WIDTH = 128
ADAPTER_RANK = 16
ADAPTER_SCALE = 2.0
EPSILON = 1e-05
ROPE_BASE = 500000.0
MESH = pl.DeviceIdType.MESH
F32 = jnp.float32
BF16 = jnp.bfloat16
GROUPS = QUERY_HEAD_COUNT // KEY_VALUE_HEADS
REQ_STEP = 8


def dot(a, b):
    return jnp.dot(a, b, preferred_element_type=F32)


def start_remote(src, dst, send, recv, axis, index):
    copy = pltpu.make_async_remote_copy(
        src_ref=src, dst_ref=dst, send_sem=send, recv_sem=recv,
        device_id={axis: index}, device_id_type=MESH,
    )
    copy.start()
    return copy


def kernel(
    n, n_tp,
    hid, gain, ids_row, ids_col, fill, cosine, sine,
    qw_h, kw_h, vw_h, ow_h, dw_h, qu_h, vu_h, kc_h, vc_h,
    out, nk_out, nv_out,
    qw, kw, vw, ow, dw, qu, vu, kc, vc,
    normed, route, rin, xin, xnorm, inv, shr, shr_in, tsend, term, rs, rq3, nk3, nv3, ctx3, ctx,
    osend, oterm, opair, osum, oown, ors,
    load_sem, route_s, route_r, x_s, x_r, pair_s, pair_r, inv_s, inv_r, shr_s, shr_r, rs_s, rs_r,
    ctx_s, ctx_r, out_s, out_r, far_s, far_r,
):
    a = lax.axis_index("ada")
    t = lax.axis_index("tp")
    core = lax.rem(t, 2)
    partner = t + 1 - 2 * core
    rows, model = hid.shape
    cap = route.shape[1]
    t_width = dw.shape[0]
    s_width = xin.shape[1]
    half = s_width // 2
    q_width, kv_width = qw.shape[1], kw.shape[1]
    share = oown.shape[0]
    chips = n_tp // 2
    chip = t // 2
    ranks2 = dw.shape[1]
    held = ranks2 // (2 * ADAPTER_RANK)

    loads = [
        pltpu.make_async_copy(src, dst, load_sem.at[i])
        for i, (src, dst) in enumerate(
            [(dw_h, dw), (qu_h, qu), (vu_h, vu), (kw_h, kw), (vw_h, vw), (qw_h, qw), (kc_h, kc), (vc_h, vc), (ow_h, ow)]
        )
    ]
    for load in loads:
        load.start()

    barrier = pltpu.get_barrier_semaphore()
    for d in range(1, n):
        pl.semaphore_signal(barrier, inc=1, device_id={"ada": lax.rem(a + d, n)}, device_id_type=MESH)
    for d in range(1, n_tp):
        pl.semaphore_signal(barrier, inc=1, device_id={"tp": lax.rem(t + d, n_tp)}, device_id_type=MESH)

    my_half = pl.ds(pl.multiple_of(core * half, 128), half)
    my_rows = pl.ds(pl.multiple_of(a * rows, rows), rows)
    pl.semaphore_wait(barrier, n - 1 + n_tp - 1)
    x_copies = []
    for d in range(1, n):
        to = lax.rem(a + d, n)
        x_copies.append(
            start_remote(
                hid.at[:, pl.ds(pl.multiple_of(to * s_width + core * half, 128), half)],
                xin.at[my_rows, my_half], x_s.at[d - 1], x_r.at[d - 1], "ada", to,
            )
        )

    step = 1024
    squares = jnp.zeros((rows, 1), F32)
    for c in range(0, model, step):
        wide = hid[:, c : c + step].astype(F32)
        squares = squares + jnp.sum(wide * wide, axis=-1, keepdims=True)
    inverse = lax.rsqrt(squares / model + EPSILON)
    diagonal = lax.broadcasted_iota(jnp.int32, (rows, 128), 0) == lax.broadcasted_iota(jnp.int32, (rows, 128), 1)
    inv[a] = jnp.broadcast_to(
        jnp.sum(jnp.where(diagonal, inverse, 0.0), axis=0, keepdims=True), (8, 128)
    )
    inv_copies = []
    for d in range(1, n):
        to = lax.rem(a + d, n)
        inv_copies.append(start_remote(inv.at[a], inv.at[a], inv_s.at[d - 1], inv_r.at[d - 1], "ada", to))
    for c in range(0, model, step):
        wide = hid[:, c : c + step].astype(F32)
        normed[:, c : c + step] = (wide * inverse * gain[:, c : c + step].astype(F32)).astype(BF16)

    row_id, col_id = ids_row[...], ids_col[...]
    owner_row, owner_col = jnp.zeros_like(row_id), jnp.zeros_like(col_id)
    for o in range(1, n):
        owner_row = owner_row + (row_id >= o * held).astype(jnp.int32)
        owner_col = owner_col + (col_id >= o * held).astype(jnp.int32)
    before = lax.broadcasted_iota(jnp.int32, (rows, rows), 0) < lax.broadcasted_iota(jnp.int32, (rows, rows), 1)
    slot_row = jnp.sum(
        jnp.where((owner_col == owner_row) & before, 1.0, 0.0), axis=0, keepdims=True
    ).astype(jnp.int32)
    target = owner_row * cap + slot_row
    picker = jnp.where(
        lax.broadcasted_iota(jnp.int32, (n * cap, rows), 0) == target, 1.0, 0.0
    ).astype(BF16)
    first_col = (col_id - owner_col * held) * (2 * ADAPTER_RANK)
    lane = lax.broadcasted_iota(jnp.int32, (rows, ranks2), 1)
    colmask = jnp.where((lane >= first_col) & (lane < first_col + 2 * ADAPTER_RANK), 1.0, 0.0).astype(BF16)
    eye = jnp.where(diagonal, 1.0, 0.0).astype(BF16)
    mine = normed[:, pl.ds(pl.multiple_of(t * t_width, 128), t_width)]
    route[:, :, 0:t_width] = dot(picker, mine).astype(BF16).reshape(n, cap, t_width)
    route[:, :, t_width : t_width + ranks2] = dot(picker, colmask).astype(BF16).reshape(n, cap, ranks2)
    route[:, :, t_width + ranks2 :] = dot(picker, eye).astype(BF16).reshape(n, cap, 128)
    rin[a] = route[a]
    xin[my_rows, :] = hid[:, pl.ds(pl.multiple_of(a * s_width, 128), s_width)]

    pending = []
    for d in range(1, n):
        to = lax.rem(a + d, n)
        pending.append(start_remote(route.at[to], rin.at[a], route_s.at[d - 1], route_r.at[d - 1], "ada", to))

    pair_copies = []
    for d in range(1, n):
        source = lax.rem(a + n - d, n)
        x_copies[d - 1].wait_recv()
        region = xin.at[pl.ds(pl.multiple_of(source * rows, rows), rows), my_half]
        pair_copies.append(start_remote(region, region, pair_s.at[d - 1], pair_r.at[d - 1], "tp", partner))
    for copy in inv_copies + pair_copies:
        copy.wait_recv()
    gains = gain[:, pl.ds(pl.multiple_of(a * s_width, 128), s_width)].astype(F32)
    for s in range(n):
        column = jnp.sum(jnp.where(diagonal, inv[s, 0:1, :], 0.0), axis=-1, keepdims=True)
        block = slice(s * rows, (s + 1) * rows)
        xnorm[block, :] = (xin[block, :].astype(F32) * column * gains).astype(BF16)
    for load in loads[3:6]:
        load.wait()

    rs_copies = []

    def give(value, at, width, index):
        term[:, at : at + width] = value
        tsend[:, at : at + width] = value.astype(BF16)
        for d in range(1, n):
            to = lax.rem(a + d, n)
            rs_copies.append(
                start_remote(
                    tsend.at[pl.ds(pl.multiple_of(to * rows, rows), rows), pl.ds(at, width)],
                    rs.at[d - 1, :, pl.ds(at, width)], rs_s.at[index, d - 1], rs_r.at[index, d - 1], "ada", to,
                )
            )

    x = xnorm[...]
    give(dot(x, kw[...]), q_width, kv_width, 0)

    for load in loads[:3]:
        load.wait()
    for copy in pending:
        copy.wait_recv()
    shr[...] = dot(rin[:, :, 0:t_width].reshape(n * cap, t_width), dw[...])
    shr_copies = []
    for d in range(1, n_tp):
        to = lax.rem(t + d, n_tp)
        shr_copies.append(start_remote(shr, shr_in.at[d - 1], shr_s.at[d - 1], shr_r.at[d - 1], "tp", to))
    for copy in shr_copies:
        copy.wait_recv()
    total = shr[...]
    for d in range(1, n_tp):
        total = total + shr_in[d - 1]
    mask = rin[:, :, t_width : t_width + ranks2].reshape(n * cap, ranks2).astype(F32)
    chosen = (jnp.where(mask > 0.5, total, 0.0).astype(BF16).astype(F32) * ADAPTER_SCALE).astype(BF16)
    ups = []
    for offset in (0, ADAPTER_RANK):
        narrow = held * ADAPTER_RANK
        r_i = lax.broadcasted_iota(jnp.int32, (ranks2, narrow), 0)
        c_i = lax.broadcasted_iota(jnp.int32, (ranks2, narrow), 1)
        want = c_i + (c_i // ADAPTER_RANK) * ADAPTER_RANK + offset
        moved = dot(chosen, jnp.where(r_i == want, 1.0, 0.0).astype(BF16)).astype(BF16)
        placed = []
        for s in range(n):
            where_to = rin[s, :, t_width + ranks2 :]
            spread = lax.dot_general(
                where_to, moved[s * cap : (s + 1) * cap], (((0,), (0,)), ((), ())), preferred_element_type=F32
            )
            placed.append(spread[:rows])
        ups.append(jnp.concatenate(placed, axis=0).astype(BF16))

    give(dot(x, vw[...]) + dot(ups[1], vu[...]), q_width + kv_width, kv_width, 1)
    q_step = min(512, q_width)
    for i in range(q_width // q_step):
        at = i * q_step
        give(
            dot(x, qw[:, at : at + q_step]) + dot(ups[0], qu[:, at : at + q_step]), at, q_step, 2 + i
        )

    cos_v, sin_v = cosine[...], sine[...]

    def summed(at, width):
        value = term[my_rows, at : at + width]
        for d in range(1, n):
            value = value + rs[d - 1, :, at : at + width].astype(F32)
        return value

    def turn(value):
        return (value * cos_v + pltpu.roll(value, HEAD_WIDTH // 2, 1) * sin_v).astype(BF16)

    def arrived(index):
        for copy in rs_copies[index * (n - 1) : (index + 1) * (n - 1)]:
            copy.wait_recv()

    kv_heads = kv_width // HEAD_WIDTH
    arrived(0)
    for h in range(kv_heads):
        cols = slice(h * HEAD_WIDTH, (h + 1) * HEAD_WIDTH)
        key = turn(summed(q_width + h * HEAD_WIDTH, HEAD_WIDTH))
        nk_out[:, cols] = key
        nk3[:, h, :] = key.astype(F32)
    arrived(1)
    for h in range(kv_heads):
        cols = slice(h * HEAD_WIDTH, (h + 1) * HEAD_WIDTH)
        fresh = summed(q_width + kv_width + h * HEAD_WIDTH, HEAD_WIDTH).astype(BF16)
        nv_out[:, cols] = fresh
        nv3[:, h, :] = fresh.astype(F32)
    score_scale = HEAD_WIDTH ** (-0.5)

    def attend(g, first):
        score_list, own_list, fill_list, val_list = [], [], [], []
        for j in range(REQ_STEP):
            r = first + j
            q = rq3[r, g * GROUPS : (g + 1) * GROUPS, :]
            keys = kc[r, :, g * HEAD_WIDTH : (g + 1) * HEAD_WIDTH]
            score_list.append(
                lax.dot_general(q.astype(BF16), keys, (((1,), (1,)), ((), ())), preferred_element_type=F32)
            )
            own_list.append(jnp.sum(q * nk3[r, g : g + 1, :], axis=-1, keepdims=True))
            val_list.append(jnp.broadcast_to(nv3[r, g : g + 1, :], (GROUPS, HEAD_WIDTH)))
            fill_list.append(jnp.full((GROUPS, 1), fill[r], jnp.int32))
        scores = jnp.concatenate(score_list, axis=0) * score_scale
        own = jnp.concatenate(own_list, axis=0) * score_scale
        lengths = jnp.concatenate(fill_list, axis=0)
        inside = lax.broadcasted_iota(jnp.int32, scores.shape, 1) < lengths
        masked = jnp.where(inside, scores, -1e30)
        top = jnp.maximum(jnp.max(masked, axis=-1, keepdims=True), own)
        terms = jnp.where(inside, jnp.exp(masked - top), 0.0)
        own_exp = jnp.exp(own - top)
        scale = 1.0 / (jnp.sum(terms, axis=-1, keepdims=True) + own_exp)
        low = (terms * scale).astype(BF16)
        own_part = (own_exp * scale).astype(BF16).astype(F32) * jnp.concatenate(val_list, axis=0)
        for j in range(REQ_STEP):
            r = first + j
            values = vc[r, :, g * HEAD_WIDTH : (g + 1) * HEAD_WIDTH]
            b = slice(j * GROUPS, (j + 1) * GROUPS)
            ctx3[r, g * GROUPS : (g + 1) * GROUPS, :] = dot(low[b], values) + own_part[b]

    ctx_copies = []
    turned = 0
    for g in range(kv_heads):
        while turned * HEAD_WIDTH < (g + 1) * GROUPS * HEAD_WIDTH:
            if turned * HEAD_WIDTH % q_step == 0:
                arrived(2 + turned * HEAD_WIDTH // q_step)
            rq3[:, turned, :] = turn(summed(turned * HEAD_WIDTH, HEAD_WIDTH)).astype(F32)
            turned += 1
        if g == 0:
            for load in loads[6:8]:
                load.wait()

        @pl.loop(0, rows // REQ_STEP)
        def _(i):
            attend(g, i * REQ_STEP)

        for h in range(g * GROUPS, (g + 1) * GROUPS):
            ctx[my_rows, h * HEAD_WIDTH : (h + 1) * HEAD_WIDTH] = ctx3[:, h, :].astype(BF16)
        here = ctx.at[my_rows, pl.ds(g * GROUPS * HEAD_WIDTH, GROUPS * HEAD_WIDTH)]
        for d in range(1, n):
            to = lax.rem(a + d, n)
            ctx_copies.append(start_remote(here, here, ctx_s.at[g, d - 1], ctx_r.at[g, d - 1], "ada", to))
    loads[8].wait()
    for copy in ctx_copies:
        copy.wait_recv()

    o_step = min(512, s_width)
    out_copies = []
    every = ctx[...]
    for i in range(s_width // o_step):
        at = i * o_step
        value = dot(every, ow[:, at : at + o_step])
        oterm[:, at : at + o_step] = value
        osend[:, at : at + o_step] = value.astype(BF16)
        for j in range(chips):
            out_copies.append(
                start_remote(
                    osend.at[pl.ds(pl.multiple_of((2 * j + 1 - core) * share, share), share), pl.ds(at, o_step)],
                    opair.at[j, :, pl.ds(at, o_step)], out_s.at[i, j], out_r.at[i, j], "tp", partner,
                )
            )

    far_copies = []
    for i in range(s_width // o_step):
        cols = slice(i * o_step, (i + 1) * o_step)
        for copy in out_copies[i * chips : (i + 1) * chips]:
            copy.wait_recv()
        for e in range(1, chips):
            to = lax.rem(chip + e, chips)
            there = pl.ds(pl.multiple_of((2 * to + core) * share, share), share)
            osum[e - 1, :, cols] = (oterm[there, cols] + opair[to, :, cols].astype(F32)).astype(BF16)
            far_copies.append(
                start_remote(
                    osum.at[e - 1, :, pl.ds(i * o_step, o_step)], ors.at[e - 1, :, pl.ds(i * o_step, o_step)],
                    far_s.at[i, e - 1], far_r.at[i, e - 1], "tp", 2 * to + core,
                )
            )

    out_rows = pl.ds(pl.multiple_of(t * share, share), share)
    for i in range(s_width // o_step):
        cols = slice(i * o_step, (i + 1) * o_step)
        oown[:, cols] = (
            xin[out_rows, cols].astype(F32) + (oterm[out_rows, cols] + opair[chip, :, cols].astype(F32))
        )
    for i in range(s_width // o_step):
        cols = slice(i * o_step, (i + 1) * o_step)
        for copy in far_copies[i * (chips - 1) : (i + 1) * (chips - 1)]:
            copy.wait_recv()
        value = oown[:, cols]
        for e in range(1, chips):
            value = value + ors[e - 1, :, cols].astype(F32)
        out[:, cols] = value.astype(BF16)

    for copy in (
        pending + x_copies + inv_copies + shr_copies + pair_copies + rs_copies + ctx_copies + out_copies + far_copies
    ):
        copy.wait_send()


def on_device(
    n, n_tp, hidden, input_norm_gain, request_adapter, cache_fill_length, query_weight, key_weight,
    value_weight, output_weight, down_weight_all, query_up_weight, value_up_weight,
    rotated_key_cache, stored_value_cache,
):
    rows, model = hidden.shape
    q_width, kv_width = query_weight.shape[1], key_weight.shape[1]
    s_width, t_width = query_weight.shape[0], down_weight_all.shape[0]
    ranks2 = down_weight_all.shape[1]
    cap = max(2, (2 * rows + n - 1) // n)
    cap = (cap + 15) // 16 * 16
    share = n * rows // n_tp
    chips = n_tp // 2
    total = q_width + 2 * kv_width
    kv_heads, heads = kv_width // HEAD_WIDTH, q_width // HEAD_WIDTH
    halfway = HEAD_WIDTH // 2
    frequency = ROPE_BASE ** (-2.0 * jnp.arange(halfway, dtype=F32) / HEAD_WIDTH)
    angles = cache_fill_length.astype(F32)[:, None] * frequency[None, :]
    cosine, sine = jnp.cos(angles), jnp.sin(angles)
    cosine = jnp.concatenate([cosine, cosine], axis=1)
    sine = jnp.concatenate([-sine, sine], axis=1)
    big = [query_weight, key_weight, value_weight, output_weight, down_weight_all, query_up_weight,
           value_up_weight, rotated_key_cache, stored_value_cache]
    chunks = 2 + q_width // min(512, q_width)
    o_chunks = s_width // min(512, s_width)
    vmem = pl.BlockSpec(memory_space=pltpu.VMEM)
    dma = pltpu.SemaphoreType.DMA
    v = pltpu.VMEM
    scratch = [v(w.shape, w.dtype) for w in big] + [
        v((rows, model), BF16),
        v((n, cap, t_width + ranks2 + 128), BF16),
        v((n, cap, t_width + ranks2 + 128), BF16),
        v((n * rows, s_width), BF16),
        v((n * rows, s_width), BF16),
        v((n, 8, 128), F32),
        v((n * cap, ranks2), F32),
        v((n_tp - 1, n * cap, ranks2), F32),
        v((n * rows, total), BF16),
        v((n * rows, total), F32),
        v((n - 1, rows, total), BF16),
        v((rows, heads, HEAD_WIDTH), F32),
        v((rows, kv_heads, HEAD_WIDTH), F32),
        v((rows, kv_heads, HEAD_WIDTH), F32),
        v((rows, heads, HEAD_WIDTH), F32),
        v((n * rows, q_width), BF16),
        v((n * rows, s_width), BF16),
        v((n * rows, s_width), F32),
        v((chips, share, s_width), BF16),
        v((chips - 1, share, s_width), BF16),
        v((share, s_width), F32),
        v((chips - 1, share, s_width), BF16),
        dma((9,)),
        dma((n - 1,)), dma((n - 1,)),
        dma((n - 1,)), dma((n - 1,)),
        dma((n - 1,)), dma((n - 1,)),
        dma((n - 1,)), dma((n - 1,)),
        dma((n_tp - 1,)), dma((n_tp - 1,)),
        dma((chunks, n - 1)), dma((chunks, n - 1)),
        dma((kv_heads, n - 1)), dma((kv_heads, n - 1)),
        dma((o_chunks, chips)), dma((o_chunks, chips)),
        dma((o_chunks, chips - 1)), dma((o_chunks, chips - 1)),
    ]
    return tuple(
        pl.pallas_call(
            functools.partial(kernel, n, n_tp),
            out_shape=[
                jax.ShapeDtypeStruct((share, s_width), BF16),
                jax.ShapeDtypeStruct((rows, kv_width), BF16),
                jax.ShapeDtypeStruct((rows, kv_width), BF16),
            ],
            in_specs=[vmem] * 4 + [pl.BlockSpec(memory_space=pltpu.SMEM)] + [vmem] * 2
            + [pl.BlockSpec(memory_space=pl.ANY)] * 9,
            out_specs=[vmem] * 3,
            scratch_shapes=scratch,
            compiler_params=pltpu.CompilerParams(
                collective_id=0, has_side_effects=True, vmem_limit_bytes=63 * 1024 * 1024
            ),
        )(
            hidden, input_norm_gain[None, :], request_adapter[None, :], request_adapter[:, None],
            cache_fill_length, cosine, sine, *big,
        )
    )


def solution(mesh):
    return jax.shard_map(
        functools.partial(on_device, mesh.shape["ada"], mesh.shape["tp"]),
        mesh=mesh,
        in_specs=(
            P(("rep", "ada"), None),
            P(),
            P(("rep", "ada")),
            P(("rep", "ada")),
            P("ada", "tp"),
            P("ada", "tp"),
            P("ada", "tp"),
            P("tp", "ada"),
            P("tp", "ada"),
            P("ada", "tp"),
            P("ada", "tp"),
            P(("rep", "ada"), None, "tp"),
            P(("rep", "ada"), None, "tp"),
        ),
        out_specs=(P(("rep", "tp"), "ada"), P(("rep", "ada"), "tp"), P(("rep", "ada"), "tp")),
        check_vma=False,
    )
```

profile of v0, /device:TPU:0, one launch (start us, length us, event | category | flops | bytes accessed | tf_op | source)
XLA Modules:
  0.0 67.2 jit_solution(5840831443805799616)
XLA Ops:
  0.6 0.7 convert_element_type.3
  1.3 1.3 %copy.16.ids_col = s32[32,1]{1,0:T(8,128)} copy(s32[32,1]{0,1:T(1,128)} %bitcast.2) | data formatting | bytes 256 | tf_op jit(solution)/shard_map/broadcast_in_dim | solution.py:428
  2.6 1.3 %broadcast_in_dim.11.gain = bf16[1,8192]{1,0:T(2,128)(2,1)} reshape(bf16[8192]{0:T(1024)(128)(2,1)} %param.14) | data formatting | bytes 32768 | tf_op jit(solution)/shard_map/broadcast_in_dim | solution.py:428
  4.0 0.1 fusion
  4.1 0.7 %pad_maximum_fusion = (f32[32,128]{1,0:T(8,128)}, f32[32,128]{1,0:T(8,128)}) fusion(f32[32,64]{1,0:T(8,128)S(1)} %get-tuple-element.5, f32[32,64]{1,0:T(8,128)S(1)} %get-tuple-element.4, f32[32,64]{1,0:T(8,128)S(1)} %get-tuple-element.3), kind=kLoop, calls=%fused_computation.2 | loop fusion | flops 8192 | bytes 57344 | tf_op jit(solution)/shard_map/concatenate | solution.py:369
  4.8 58.1 %shard_map.148 = (bf16[32,2048]{1,0:T(8,128)(2,1)}, bf16[32,256]{1,0:T(8,128)(2,1)}, bf16[32,256]{1,0:T(8,128)(2,1)}) custom-call(bf16[32,8192]{1,0:T(8,128)(2,1)} %hid.1, bf16[1,8192]{1,0:T(2,128)(2,1)} %broadcast_in_dim.11.gain, s32[1,32]{1,0:T(1,128)} %bitcast.3, s32[32,1]{1,0:T(8,128)} %copy.16.ids_col, s32[32]{0:T(128)} %fill.1, ...), custom_call_target="tpu_custom_call" | custom-call | tf_op jit(solution)/shard_map/pallas_call | solution.py:413
  63.0 1.6 %copy.20 = bf16[32,2048]{1,0:T(8,128)(2,1)} copy(bf16[32,2048]{1,0:T(8,128)(2,1)} %get-tuple-element.11) | data formatting | bytes 262144
  64.5 1.3 %copy.21 = bf16[32,256]{1,0:T(8,128)(2,1)} copy(bf16[32,256]{1,0:T(8,128)(2,1)} %get-tuple-element.12) | data formatting | bytes 32768
  65.9 1.3 %copy.22 = bf16[32,256]{1,0:T(8,128)(2,1)} copy(bf16[32,256]{1,0:T(8,128)(2,1)} %get-tuple-element.13) | data formatting | bytes 32768
  (1 shorter events, 0.0 us)
where the time goes:
time: 67.7 us; the launch traced here: 67.2 us
  Pallas kernels  58.1 us (86%)
  local copies, waits for them, and re-layouts  6.91 us (10%)
  other arithmetic  1.51 us (2%)
    pallas_call x1, Pallas kernels, on_device(): pl.pallas_call(functools.partial(kernel, n, n_tp), out_shape=[jax.ShapeDt...  58.1 us
    unnamed x3, local copies, waits for them, and re-layouts  4.21 us

commit v1 on v0

--- a/solution.py
+++ b/solution.py
@@ -2,6 +2,7 @@
 
 import jax
 import jax.numpy as jnp
+import numpy as np
 from jax import lax
 from jax.experimental import pallas as pl
 from jax.experimental.pallas import tpu as pltpu
@@ -36,13 +37,13 @@
 
 def kernel(
     n, n_tp,
-    hid, gain, ids_row, ids_col, fill, cosine, sine,
+    hid_h, gain, ids_row, fill, fill_row, freq,
     qw_h, kw_h, vw_h, ow_h, dw_h, qu_h, vu_h, kc_h, vc_h,
     out, nk_out, nv_out,
-    qw, kw, vw, ow, dw, qu, vu, kc, vc,
-    normed, route, rin, xin, xnorm, inv, shr, shr_in, tsend, term, rs, rq3, nk3, nv3, ctx3, ctx,
+    hid, qw, kw, vw, ow, dw, qu, vu, kc, vc,
+    wide_gain, normed, route, rin, xin, xnorm, inv, shr, shr_in, tsend, term, rs, rq3, nk3, nv3, ctx3, ctx,
     osend, oterm, opair, osum, oown, ors,
-    load_sem, route_s, route_r, x_s, x_r, pair_s, pair_r, inv_s, inv_r, shr_s, shr_r, rs_s, rs_r,
+    hid_sem, load_sem, route_s, route_r, x_s, x_r, pair_s, pair_r, inv_s, inv_r, shr_s, shr_r, rs_s, rs_r,
     ctx_s, ctx_r, out_s, out_r, far_s, far_r,
 ):
     a = lax.axis_index("ada")
@@ -61,14 +62,14 @@
     ranks2 = dw.shape[1]
     held = ranks2 // (2 * ADAPTER_RANK)
 
+    hid_load = pltpu.make_async_copy(hid_h, hid, hid_sem)
+    hid_load.start()
     loads = [
         pltpu.make_async_copy(src, dst, load_sem.at[i])
         for i, (src, dst) in enumerate(
             [(dw_h, dw), (qu_h, qu), (vu_h, vu), (kw_h, kw), (vw_h, vw), (qw_h, qw), (kc_h, kc), (vc_h, vc), (ow_h, ow)]
         )
     ]
-    for load in loads:
-        load.start()
 
     barrier = pltpu.get_barrier_semaphore()
     for d in range(1, n):
@@ -76,6 +77,22 @@
     for d in range(1, n_tp):
         pl.semaphore_signal(barrier, inc=1, device_id={"tp": lax.rem(t + d, n_tp)}, device_id_type=MESH)
 
+    for load in loads:
+        load.start()
+    wide_gain[...] = gain[...].astype(F32)
+    diagonal = lax.broadcasted_iota(jnp.int32, (rows, 128), 0) == lax.broadcasted_iota(jnp.int32, (rows, 128), 1)
+    square = diagonal[:, :rows]
+
+    def to_column(row):
+        return jnp.sum(jnp.where(square, row, 0.0), axis=-1, keepdims=True)
+
+    row_id = ids_row[...]
+    col_id = to_column(row_id.astype(F32)).astype(jnp.int32)
+    angles = to_column(fill_row[...].astype(F32)) * freq[...]
+    cos_v, sin_v = jnp.cos(angles), jnp.sin(angles)
+    sin_v = jnp.where(lax.broadcasted_iota(jnp.int32, sin_v.shape, 1) < HEAD_WIDTH // 2, -sin_v, sin_v)
+
+    hid_load.wait()
     my_half = pl.ds(pl.multiple_of(core * half, 128), half)
     my_rows = pl.ds(pl.multiple_of(a * rows, rows), rows)
     pl.semaphore_wait(barrier, n - 1 + n_tp - 1)
@@ -89,13 +106,13 @@
             )
         )
 
-    step = 1024
-    squares = jnp.zeros((rows, 1), F32)
+    step = 128
+    squares = jnp.zeros((rows, step), F32)
     for c in range(0, model, step):
         wide = hid[:, c : c + step].astype(F32)
-        squares = squares + jnp.sum(wide * wide, axis=-1, keepdims=True)
+        squares = squares + wide * wide
+    squares = jnp.sum(squares, axis=-1, keepdims=True)
     inverse = lax.rsqrt(squares / model + EPSILON)
-    diagonal = lax.broadcasted_iota(jnp.int32, (rows, 128), 0) == lax.broadcasted_iota(jnp.int32, (rows, 128), 1)
     inv[a] = jnp.broadcast_to(
         jnp.sum(jnp.where(diagonal, inverse, 0.0), axis=0, keepdims=True), (8, 128)
     )
@@ -105,9 +122,8 @@
         inv_copies.append(start_remote(inv.at[a], inv.at[a], inv_s.at[d - 1], inv_r.at[d - 1], "ada", to))
     for c in range(0, model, step):
         wide = hid[:, c : c + step].astype(F32)
-        normed[:, c : c + step] = (wide * inverse * gain[:, c : c + step].astype(F32)).astype(BF16)
-
-    row_id, col_id = ids_row[...], ids_col[...]
+        normed[:, c : c + step] = (wide * inverse * wide_gain[c // step : c // step + 1, :]).astype(BF16)
+
     owner_row, owner_col = jnp.zeros_like(row_id), jnp.zeros_like(col_id)
     for o in range(1, n):
         owner_row = owner_row + (row_id >= o * held).astype(jnp.int32)
@@ -144,11 +160,12 @@
         pair_copies.append(start_remote(region, region, pair_s.at[d - 1], pair_r.at[d - 1], "tp", partner))
     for copy in inv_copies + pair_copies:
         copy.wait_recv()
-    gains = gain[:, pl.ds(pl.multiple_of(a * s_width, 128), s_width)].astype(F32)
     for s in range(n):
         column = jnp.sum(jnp.where(diagonal, inv[s, 0:1, :], 0.0), axis=-1, keepdims=True)
         block = slice(s * rows, (s + 1) * rows)
-        xnorm[block, :] = (xin[block, :].astype(F32) * column * gains).astype(BF16)
+        for c in range(0, s_width, step):
+            gains = wide_gain[pl.ds(a * (s_width // step) + c // step, 1), :]
+            xnorm[block, c : c + step] = (xin[block, c : c + step].astype(F32) * column * gains).astype(BF16)
     for load in loads[3:6]:
         load.wait()
 
@@ -209,8 +226,6 @@
             dot(x, qw[:, at : at + q_step]) + dot(ups[0], qu[:, at : at + q_step]), at, q_step, 2 + i
         )
 
-    cos_v, sin_v = cosine[...], sine[...]
-
     def summed(at, width):
         value = term[my_rows, at : at + width]
         for d in range(1, n):
@@ -363,11 +378,8 @@
     total = q_width + 2 * kv_width
     kv_heads, heads = kv_width // HEAD_WIDTH, q_width // HEAD_WIDTH
     halfway = HEAD_WIDTH // 2
-    frequency = ROPE_BASE ** (-2.0 * jnp.arange(halfway, dtype=F32) / HEAD_WIDTH)
-    angles = cache_fill_length.astype(F32)[:, None] * frequency[None, :]
-    cosine, sine = jnp.cos(angles), jnp.sin(angles)
-    cosine = jnp.concatenate([cosine, cosine], axis=1)
-    sine = jnp.concatenate([-sine, sine], axis=1)
+    frequency = np.float32(ROPE_BASE) ** (np.float32(-2.0) * np.arange(halfway, dtype=np.float32) / np.float32(HEAD_WIDTH))
+    frequency = jnp.asarray(np.concatenate([frequency, frequency])[None, :])
     big = [query_weight, key_weight, value_weight, output_weight, down_weight_all, query_up_weight,
            value_up_weight, rotated_key_cache, stored_value_cache]
     chunks = 2 + q_width // min(512, q_width)
@@ -375,7 +387,9 @@
     vmem = pl.BlockSpec(memory_space=pltpu.VMEM)
     dma = pltpu.SemaphoreType.DMA
     v = pltpu.VMEM
-    scratch = [v(w.shape, w.dtype) for w in big] + [
+    lanes = 128
+    scratch = [v(hidden.shape, hidden.dtype)] + [v(w.shape, w.dtype) for w in big] + [
+        v((model // lanes, lanes), F32),
         v((rows, model), BF16),
         v((n, cap, t_width + ranks2 + 128), BF16),
         v((n, cap, t_width + ranks2 + 128), BF16),
@@ -398,7 +412,7 @@
         v((chips - 1, share, s_width), BF16),
         v((share, s_width), F32),
         v((chips - 1, share, s_width), BF16),
-        dma((9,)),
+        dma, dma((9,)),
         dma((n - 1,)), dma((n - 1,)),
         dma((n - 1,)), dma((n - 1,)),
         dma((n - 1,)), dma((n - 1,)),
@@ -409,26 +423,22 @@
         dma((o_chunks, chips)), dma((o_chunks, chips)),
         dma((o_chunks, chips - 1)), dma((o_chunks, chips - 1)),
     ]
-    return tuple(
-        pl.pallas_call(
-            functools.partial(kernel, n, n_tp),
-            out_shape=[
-                jax.ShapeDtypeStruct((share, s_width), BF16),
-                jax.ShapeDtypeStruct((rows, kv_width), BF16),
-                jax.ShapeDtypeStruct((rows, kv_width), BF16),
-            ],
-            in_specs=[vmem] * 4 + [pl.BlockSpec(memory_space=pltpu.SMEM)] + [vmem] * 2
-            + [pl.BlockSpec(memory_space=pl.ANY)] * 9,
-            out_specs=[vmem] * 3,
-            scratch_shapes=scratch,
-            compiler_params=pltpu.CompilerParams(
-                collective_id=0, has_side_effects=True, vmem_limit_bytes=63 * 1024 * 1024
-            ),
-        )(
-            hidden, input_norm_gain[None, :], request_adapter[None, :], request_adapter[:, None],
-            cache_fill_length, cosine, sine, *big,
-        )
+    shapes = [((share, s_width), BF16), ((rows, kv_width), BF16), ((rows, kv_width), BF16)]
+    held = pl.pallas_call(
+        functools.partial(kernel, n, n_tp),
+        out_shape=[pltpu.VMEM(*one) for one in shapes],
+        in_specs=[pl.BlockSpec(memory_space=pl.ANY)] + [vmem] * 2 + [pl.BlockSpec(memory_space=pltpu.SMEM)] + [vmem] * 2
+        + [pl.BlockSpec(memory_space=pl.ANY)] * 9,
+        out_specs=[vmem] * 3,
+        scratch_shapes=scratch,
+        compiler_params=pltpu.CompilerParams(
+            collective_id=0, has_side_effects=True, vmem_limit_bytes=62 * 1024 * 1024
+        ),
+    )(
+        hidden, input_norm_gain.reshape(model // lanes, lanes), request_adapter[None, :],
+        cache_fill_length, cache_fill_length[None, :], frequency, *big,
     )
+    return tuple(held)
 
 
 def solution(mesh):

time: 67.7 us -> 60 us (0.89)
  local copies, waits for them, and re-layouts: 6.91 us -> 1.87 us
  other arithmetic: 1.51 us -> 0 us
  Pallas kernels: 58.1 us -> 57.2 us
    broadcast_in_dim x2 -> x0, local copies, waits for them, and re-layouts: 2.69 us -> none  [the longest x1 1.35 us: on_device(): input_norm_gain[None, :]]
    unnamed x3, local copies, waits for them, and re-layouts: 4.21 us -> 1.87 us
    pallas_call x1, Pallas kernels: 58.1 us -> 57.2 us  [on_device(): pl.pallas_call(functools.partial(kernel, n, n_tp), out_shape=[pltpu.VMEM(...]
    concatenate x1 -> x0, other arithmetic: 0.7 us -> none  [on_device(): cosine = jnp.concatenate([cosine, cosine], axis=1)]
where the time goes in v1:
time: 60 us; the launch traced here: 59.7 us
  Pallas kernels  57.2 us (95%)
  local copies, waits for them, and re-layouts  1.87 us (3%)
  between operations  0.64 us (1%)
    pallas_call x1, Pallas kernels, on_device(): pl.pallas_call(functools.partial(kernel, n, n_tp), out_shape=[pltpu.VMEM(...  57.2 us
    unnamed x3, local copies, waits for them, and re-layouts  1.87 us

profile of v1, /device:TPU:0, one launch (start us, length us, event | category | flops | bytes accessed | tf_op | source)
XLA Modules:
  0.0 59.7 jit_solution(12469634050759357022)
XLA Ops:
  0.6 57.2 %shard_map.157 = (bf16[32,2048]{1,0:T(8,128)(2,1)S(1)}, bf16[32,256]{1,0:T(8,128)(2,1)S(1)}, bf16[32,256]{1,0:T(8,128)(2,1)S(1)}) custom-call(bf16[32,8192]{1,0:T(8,128)(2,1)} %hid_h.1, bf16[64,128]{1,0:T(8,128)(2,1)} %bitcast.3, s32[1,32]{1,0:T(1,128)} %bitcast.5, s32[32]{0:T(128)} %fill.1, s32[1,32]{1,0:T(1,128)} %bitcast.4, f32[1,128]{1,0:T(1,128)} %constant.2.clone.freq, ...), custom_call_target="tpu_custom_call" | custom-call | tf_op jit(solution)/shard_map/pallas_call | solution.py:427
  57.9 0.7 %copy.20 = bf16[32,2048]{1,0:T(8,128)(2,1)} copy(bf16[32,2048]{1,0:T(8,128)(2,1)S(1)} %get-tuple-element.3) | data formatting | bytes 262144
  58.5 0.6 %copy.21 = bf16[32,256]{1,0:T(8,128)(2,1)} copy(bf16[32,256]{1,0:T(8,128)(2,1)S(1)} %get-tuple-element.4) | data formatting | bytes 32768
  59.1 0.6 %copy.22 = bf16[32,256]{1,0:T(8,128)(2,1)} copy(bf16[32,256]{1,0:T(8,128)(2,1)S(1)} %get-tuple-element.5) | data formatting | bytes 32768

commit v2 on v1

v2 whole, which is shorter than its diff:
```python
import functools

import jax
import jax.numpy as jnp
import numpy as np
from jax import lax
from jax.experimental import pallas as pl
from jax.experimental.pallas import tpu as pltpu
from jax.sharding import PartitionSpec as P

QUERY_HEAD_COUNT = 64
KEY_VALUE_HEADS = 8
HEAD_WIDTH = 128
ADAPTER_RANK = 16
ADAPTER_SCALE = 2.0
EPSILON = 1e-05
ROPE_BASE = 500000.0
MESH = pl.DeviceIdType.MESH
F32 = jnp.float32
BF16 = jnp.bfloat16
GROUPS = QUERY_HEAD_COUNT // KEY_VALUE_HEADS
REQ_STEP = 8


def dot(a, b):
    return jnp.dot(a, b, preferred_element_type=F32)


def remote(src, dst, send, recv, target):
    return pltpu.make_async_remote_copy(
        src_ref=src, dst_ref=dst, send_sem=send, recv_sem=recv, device_id=target, device_id_type=MESH
    )


def kernel(
    n, n_tp,
    hid_h, gain_h, ids_h, fill_h, freq_h, qw_h, kw_h, vw_h, ow_h, dw_h, qu_h, vu_h, kc_h, vc_h,
    out, nk_out, nv_out,
    hid, qw, kw, vw, ow, dw, qu, vu, kc, vc,
    gain, ids_row, fill_row, freq, fill, wide_gain, normed, meta, route, rin, xin, xnorm, shr, shr_in, tsend, term, rs, rq3, nk3, nv3, ctx3, ctx,
    osend, oterm, opair, osum, oown, ors,
    hid_sem, small_sem, load_sem, meta_s, meta_r, route_s, route_r, x_s, x_r, pair_s, pair_r, shr_s, shr_r, rs_s, rs_r,
    ctx_s, ctx_r, out_s, out_r, far_s, far_r,
):
    a = lax.axis_index("ada")
    t = lax.axis_index("tp")
    core = lax.rem(t, 2)
    partner = t + 1 - 2 * core
    rows, model = hid.shape
    cap = route.shape[1]
    t_width, ranks2 = dw.shape
    s_width = xin.shape[1]
    half = s_width // 2
    q_width, kv_width = qw.shape[1], kw.shape[1]
    kv_heads = kv_width // HEAD_WIDTH
    share = oown.shape[0]
    chips = n_tp // 2
    chip = t // 2
    pair = 2 * ADAPTER_RANK
    held = ranks2 // pair
    step = 128
    relays = n > 3

    first = 1 - lax.div(a + n - 1, n)
    last = lax.div(a + 1, n)
    upper = lax.div(2 * a, n)
    is_end = jnp.logical_and(relays, jnp.logical_or(a == 0, a == n - 1))
    is_next = jnp.logical_and(relays, jnp.logical_or(a == 1, a == n - 2))
    end = (first + last) if relays else 0

    def peer(k):
        low = n - 1 - k
        low = low - lax.div(a - low + n, n)
        high = k + lax.div(k - a + n, n)
        return low + upper * (high - low)

    def block(index, size):
        return pl.ds(pl.multiple_of(index * size, size), size)

    def when(condition, action):
        if condition is True:
            action()
        elif condition is not False:
            pl.when(condition)(action)

    hid_load = pltpu.make_async_copy(hid_h, hid, hid_sem)
    hid_load.start()
    small_loads = [
        pltpu.make_async_copy(src, dst, small_sem.at[i])
        for i, (src, dst) in enumerate(
            [(gain_h, gain), (ids_h, ids_row), (fill_h, fill_row), (freq_h, freq), (fill_h, fill)]
        )
    ]
    for load in small_loads:
        load.start()
    barrier = pltpu.get_barrier_semaphore()
    for d in range(1, n):
        pl.semaphore_signal(barrier, inc=1, device_id={"ada": lax.rem(a + d, n)}, device_id_type=MESH)
    for d in range(1, n_tp):
        pl.semaphore_signal(barrier, inc=1, device_id={"tp": lax.rem(t + d, n_tp)}, device_id_type=MESH)
    loads = [
        pltpu.make_async_copy(src, dst, load_sem.at[i])
        for i, (src, dst) in enumerate(
            [(dw_h, dw), (qu_h, qu), (vu_h, vu), (kw_h, kw), (vw_h, vw), (qw_h, qw), (kc_h, kc), (vc_h, vc), (ow_h, ow)]
        )
    ]
    for load in loads:
        load.start()

    for load in small_loads:
        load.wait()
    wide_gain[...] = gain[...].astype(F32)
    diagonal = lax.broadcasted_iota(jnp.int32, (rows, 128), 0) == lax.broadcasted_iota(jnp.int32, (rows, 128), 1)
    square = diagonal[:, :rows]
    before = lax.broadcasted_iota(jnp.int32, (rows, rows), 0) < lax.broadcasted_iota(jnp.int32, (rows, rows), 1)

    def to_column(row):
        return jnp.sum(jnp.where(square, row, 0.0), axis=-1, keepdims=True)

    def to_row(column):
        return jnp.sum(jnp.where(diagonal, column, 0.0), axis=0, keepdims=True)

    row_id = ids_row[...].astype(F32)
    col_id = to_column(row_id)
    angles = to_column(fill_row[...].astype(F32)) * freq[...]
    cos_v, sin_v = jnp.cos(angles), jnp.sin(angles)
    sin_v = jnp.where(lax.broadcasted_iota(jnp.int32, sin_v.shape, 1) < HEAD_WIDTH // 2, -sin_v, sin_v)
    owner_row, owner_col = jnp.zeros_like(row_id), jnp.zeros_like(col_id)
    for o in range(1, n):
        owner_row = owner_row + (row_id >= o * held).astype(F32)
        owner_col = owner_col + (col_id >= o * held).astype(F32)
    slot_row = jnp.sum(jnp.where((owner_col == owner_row) & before, 1.0, 0.0), axis=0, keepdims=True)
    target = (owner_row * cap + slot_row).astype(jnp.int32)
    picker = jnp.where(
        lax.broadcasted_iota(jnp.int32, (n * cap, rows), 0) == target, 1.0, 0.0
    ).astype(BF16)
    if relays:
        @pl.when(is_end)
        def _():
            rs[peer(0), :, :q_width] = jnp.zeros((rows, q_width), rs.dtype)

    hid_load.wait()
    squares = jnp.zeros((rows, step), F32)
    for c in range(0, model, step):
        wide = hid[:, c : c + step].astype(F32)
        squares = squares + wide * wide
    inverse = lax.rsqrt(jnp.sum(squares, axis=-1, keepdims=True) / model + EPSILON)
    meta[a] = jnp.where(
        lax.broadcasted_iota(jnp.int32, (8, 128), 0) == 0, to_row(inverse), to_row(col_id)
    )
    for c in range(0, model, step):
        wide = hid[:, c : c + step].astype(F32)
        normed[:, c : c + step] = (wide * inverse * wide_gain[c // step : c // step + 1, :]).astype(BF16)
    route[...] = dot(picker, normed[:, block(t, t_width)]).astype(BF16).reshape(n, cap, t_width)
    rin[a] = route[a]
    my_rows = block(a, rows)
    my_half = block(core, half)
    xin[my_rows, :] = hid[:, block(a, s_width)]

    pl.semaphore_wait(barrier, n - 1 + n_tp - 1)
    sends = []

    def go(copy):
        copy.start()
        sends.append(copy)

    for k in range(n - 1):
        to = peer(k)
        go(remote(meta.at[a], meta.at[a], meta_s.at[k], meta_r.at[a], {"ada": to}))
    for k in range(n - 1):
        to = peer(k)
        go(remote(route.at[to], rin.at[a], route_s.at[k], route_r.at[a], {"ada": to}))
    for k in range(n - 1):
        to = peer(k)
        go(
            remote(
                hid.at[:, pl.ds(pl.multiple_of(to * s_width + core * half, 128), half)],
                xin.at[my_rows, my_half], x_s.at[k], x_r.at[a], {"ada": to},
            )
        )
    near_first = [peer(k) for k in reversed(range(n - 1))]

    def landed(dst, send, recv):
        remote(dst, dst, send, recv, {"ada": lax.rem(a + 1, n)}).wait_recv()

    for s in near_first:
        landed(meta.at[s], meta_s.at[0], meta_r.at[s])
    lane_cap = lax.broadcasted_iota(jnp.int32, (cap, ranks2), 1) // pair
    lane_rows = lax.broadcasted_iota(jnp.int32, (rows, ranks2), 1) // pair
    low_id = (a * held).astype(F32)
    places, slot_masks, id_cols, scales = [], [], [], []
    for s in range(n):
        ids_s = meta[s, 1:2, :rows]
        col_s = to_column(ids_s)
        here_row = (ids_s >= low_id) & (ids_s < low_id + held)
        here_col = (col_s >= low_id) & (col_s < low_id + held)
        slots = jnp.sum(jnp.where(here_col & before, 1.0, 0.0), axis=0, keepdims=True)
        chosen_slot = lax.broadcasted_iota(jnp.int32, (cap, rows), 0) == slots.astype(jnp.int32)
        slot_id = jnp.sum(jnp.where(chosen_slot & here_row, ids_s - low_id, 0.0), axis=-1, keepdims=True)
        slot_masks.append(lane_cap == slot_id.astype(jnp.int32))
        slot_col = to_column(slots).astype(jnp.int32)
        places.append(
            jnp.where((lax.broadcasted_iota(jnp.int32, (rows, cap), 1) == slot_col) & here_col, 1.0, 0.0).astype(BF16)
        )
        id_cols.append((col_s - low_id).astype(jnp.int32))
        scales.append(to_column(meta[s, 0:1, :rows]))
    row_ids = jnp.concatenate(id_cols, axis=0)

    loads[0].wait()
    for s in near_first:
        landed(rin.at[s], route_s.at[0], route_r.at[s])
    partial = dot(rin[...].reshape(n * cap, t_width), dw[...])
    for first_s in range(0, n, held):
        tile = jnp.zeros((cap, ranks2), F32)
        for s in range(first_s, min(n, first_s + held)):
            picked = jnp.where(slot_masks[s], partial[s * cap : (s + 1) * cap], 0.0)
            folded = picked
            for i in range(1, held):
                folded = folded + pltpu.roll(picked, i * pair, 1)
            tile = jnp.where(lane_cap == s - first_s, folded, tile)
        shr[first_s // held * cap : (first_s // held + 1) * cap, :] = tile
    for d in range(1, n_tp):
        to = lax.rem(t + d, n_tp)
        go(remote(shr, shr_in.at[d - 1], shr_s.at[d - 1], shr_r.at[d - 1], {"tp": to}))

    def x_region(s):
        return xin.at[block(s, rows), my_half]

    for s in near_first:
        landed(x_region(s), x_s.at[0], x_r.at[s])
        go(remote(x_region(s), x_region(s), pair_s.at[s], pair_r.at[s], {"tp": partner}))

    for copy in sends[-(n - 1) - (n_tp - 1) : -(n - 1)]:
        copy.wait_recv()
    total = shr[...]
    for d in range(1, n_tp):
        total = total + shr_in[d - 1]
    chosen = (total.astype(BF16).astype(F32) * ADAPTER_SCALE).astype(BF16)
    spread = []
    for s in range(n):
        mine = chosen[s // held * cap : (s // held + 1) * cap]
        spread.append(jnp.where(lane_rows == s % held, dot(places[s], mine), 0.0))
    spread = jnp.concatenate(spread, axis=0).astype(BF16)
    narrow = held * ADAPTER_RANK
    from_lane = lax.broadcasted_iota(jnp.int32, (ranks2, narrow), 0) % pair
    to_lane = lax.broadcasted_iota(jnp.int32, (ranks2, narrow), 1) % ADAPTER_RANK
    own_lane = lax.broadcasted_iota(jnp.int32, (n * rows, narrow), 1) // ADAPTER_RANK == row_ids
    ups = []
    for offset in (0, ADAPTER_RANK):
        moved = dot(spread, jnp.where(from_lane == to_lane + offset, 1.0, 0.0).astype(BF16))
        ups.append(jnp.where(own_lane, moved, 0.0).astype(BF16))

    for s in near_first:
        other = xin.at[block(s, rows), block(1 - core, half)]
        landed(other, pair_s.at[s], pair_r.at[s])
    for s in range(n):
        rows_s = slice(s * rows, (s + 1) * rows)
        for c in range(0, s_width, step):
            gains = wide_gain[pl.ds(a * (s_width // step) + c // step, 1), :]
            xnorm[rows_s, c : c + step] = (xin[rows_s, c : c + step].astype(F32) * scales[s] * gains).astype(BF16)
    for load in loads[1:6]:
        load.wait()

    spare = n
    beside = first + last * (n - 2)
    far_target = peer(0) + end * (beside - peer(0))
    far_slot = a + end * (spare - a)
    chunks = []

    def chunk_copy(index, k):
        at, width = chunks[index]
        cols = pl.ds(at, width)
        to = peer(k)
        target, slot = (far_target, far_slot) if k == 0 and index > 0 else (to, a)
        return remote(
            tsend.at[block(to, rows), cols], rs.at[slot, :, cols], rs_s.at[index, k], rs_r.at[index, slot],
            {"ada": target},
        )

    def give(value, at, width):
        index = len(chunks)
        chunks.append((at, width))
        term[:, at : at + width] = value
        tsend[:, at : at + width] = value.astype(BF16)

    def ship(index, k):
        direct = k > 0 or index == 0 or not relays
        when(True if direct else jnp.logical_not(is_next), lambda: chunk_copy(index, k).start())

    def relay(index):
        if not relays:
            return
        at, width = chunks[index]
        cols = pl.ds(at, width)

        @pl.when(is_next)
        def _():
            landed(rs.at[spare, :, cols], rs_s.at[index, 0], rs_r.at[index, spare])
            there = block(peer(0), rows)
            tsend[there, cols] = (term[there, cols] + rs[spare, :, cols].astype(F32)).astype(BF16)
            remote(
                tsend.at[there, cols], rs.at[a, :, cols], rs_s.at[index, 0], rs_r.at[index, a], {"ada": peer(0)}
            ).start()

    def arrived(index):
        at, width = chunks[index]
        cols = pl.ds(at, width)
        for k in reversed(range(n - 1)):
            s = peer(k)
            when(
                jnp.logical_not(is_end) if relays and k == 0 and index > 0 else True,
                lambda: landed(rs.at[s, :, cols], rs_s.at[index, 0], rs_r.at[index, s]),
            )

    x = xnorm[...]
    give(
        jnp.concatenate([dot(x, kw[...]), dot(x, vw[...]) + dot(ups[1], vu[...])], axis=1), q_width, 2 * kv_width
    )
    for k in range(n - 1):
        ship(0, k)
    wide_g = GROUPS * HEAD_WIDTH
    q_step = min(512, wide_g)
    per_g = wide_g // q_step
    for g in range(kv_heads):
        group = range(1 + g * per_g, 1 + (g + 1) * per_g)
        for index in group:
            at = (index - 1) * q_step
            give(dot(x, qw[:, at : at + q_step]) + dot(ups[0], qu[:, at : at + q_step]), at, q_step)
            if g == 0:
                ship(index, 0)
        if g == 0:
            for k in range(1, n - 1):
                for index in group:
                    ship(index, k)
    for index in range(1, 1 + per_g):
        relay(index)
    for g in range(1, kv_heads):
        for k in range(n - 1):
            for index in range(1 + g * per_g, 1 + (g + 1) * per_g):
                ship(index, k)

    def summed(at, width):
        value = term[my_rows, at : at + width]
        for k in range(n - 1):
            value = value + rs[peer(k), :, at : at + width].astype(F32)
        return value

    def turn(value):
        return (value * cos_v + pltpu.roll(value, HEAD_WIDTH // 2, 1) * sin_v).astype(BF16)

    arrived(0)
    for h in range(kv_heads):
        cols = slice(h * HEAD_WIDTH, (h + 1) * HEAD_WIDTH)
        key = turn(summed(q_width + h * HEAD_WIDTH, HEAD_WIDTH))
        nk_out[:, cols] = key
        nk3[:, h, :] = key.astype(F32)
    for h in range(kv_heads):
        cols = slice(h * HEAD_WIDTH, (h + 1) * HEAD_WIDTH)
        fresh = summed(q_width + kv_width + h * HEAD_WIDTH, HEAD_WIDTH).astype(BF16)
        nv_out[:, cols] = fresh
        nv3[:, h, :] = fresh.astype(F32)
    score_scale = HEAD_WIDTH ** (-0.5)

    def attend(g, start):
        score_list, own_list, fill_list, val_list = [], [], [], []
        for j in range(REQ_STEP):
            r = start + j
            q = rq3[r, g * GROUPS : (g + 1) * GROUPS, :]
            keys = kc[r, :, g * HEAD_WIDTH : (g + 1) * HEAD_WIDTH]
            score_list.append(
                lax.dot_general(q.astype(BF16), keys, (((1,), (1,)), ((), ())), preferred_element_type=F32)
            )
            own_list.append(jnp.sum(q * nk3[r, g : g + 1, :], axis=-1, keepdims=True))
            val_list.append(jnp.broadcast_to(nv3[r, g : g + 1, :], (GROUPS, HEAD_WIDTH)))
            fill_list.append(jnp.full((GROUPS, 1), fill[0, r], jnp.int32))
        scores = jnp.concatenate(score_list, axis=0) * score_scale
        own = jnp.concatenate(own_list, axis=0) * score_scale
        lengths = jnp.concatenate(fill_list, axis=0)
        inside = lax.broadcasted_iota(jnp.int32, scores.shape, 1) < lengths
        masked = jnp.where(inside, scores, -1e30)
        top = jnp.maximum(jnp.max(masked, axis=-1, keepdims=True), own)
        terms = jnp.where(inside, jnp.exp(masked - top), 0.0)
        own_exp = jnp.exp(own - top)
        scale = 1.0 / (jnp.sum(terms, axis=-1, keepdims=True) + own_exp)
        low = (terms * scale).astype(BF16)
        own_part = (own_exp * scale).astype(BF16).astype(F32) * jnp.concatenate(val_list, axis=0)
        for j in range(REQ_STEP):
            r = start + j
            values = vc[r, :, g * HEAD_WIDTH : (g + 1) * HEAD_WIDTH]
            b = slice(j * GROUPS, (j + 1) * GROUPS)
            ctx3[r, g * GROUPS : (g + 1) * GROUPS, :] = dot(low[b], values) + own_part[b]

    piece = min(16, rows)
    pieces = rows // piece

    def ctx_region(s, index):
        g, p = index // pieces, index % pieces
        return ctx.at[pl.ds(pl.multiple_of(s * rows + p * piece, piece), piece), pl.ds(g * wide_g, wide_g)]

    def ctx_copy(index, k):
        return remote(
            ctx_region(a, index), ctx_region(a, index), ctx_s.at[index, k], ctx_r.at[index, a], {"ada": peer(k)}
        )

    def pass_copy(index):
        s = peer(0)
        outward = lax.div(a, n - 2) * (n - 1)
        return remote(
            ctx_region(s, index), ctx_region(s, index), ctx_s.at[index, n - 1], ctx_r.at[index, s], {"ada": outward}
        )

    def ctx_landed(s, index):
        landed(ctx_region(s, index), ctx_s.at[index, 0], ctx_r.at[index, s])

    def pass_on(index):
        if not relays:
            return

        @pl.when(is_next)
        def _():
            ctx_landed(peer(0), index)
            pass_copy(index).start()

    def gathered(index):
        for k in reversed(range(n - 1)):
            s = peer(k)
            when(
                jnp.logical_not(is_next) if relays and k == 0 else True,
                lambda: ctx_landed(s, index),
            )

    turned = 0
    for g in range(kv_heads):
        for index in range(1 + g * per_g, 1 + (g + 1) * per_g):
            arrived(index)
        while turned < (g + 1) * GROUPS:
            rq3[:, turned, :] = turn(summed(turned * HEAD_WIDTH, HEAD_WIDTH)).astype(F32)
            turned += 1
        if g < kv_heads - 1:
            for index in range(1 + (g + 1) * per_g, 1 + (g + 2) * per_g):
                relay(index)
        if g == 0:
            for load in loads[6:8]:
                load.wait()
        for p in range(pieces):
            @pl.loop(0, piece // REQ_STEP)
            def _(i):
                attend(g, p * piece + i * REQ_STEP)

            own_rows = pl.ds(pl.multiple_of(a * rows + p * piece, piece), piece)
            for h in range(g * GROUPS, (g + 1) * GROUPS):
                ctx[own_rows, h * HEAD_WIDTH : (h + 1) * HEAD_WIDTH] = ctx3[
                    p * piece : (p + 1) * piece, h, :
                ].astype(BF16)
            index = g * pieces + p
            when(jnp.logical_not(is_end) if relays else True, lambda: ctx_copy(index, 0).start())
            for k in range(1, n - 1):
                ctx_copy(index, k).start()

    loads[8].wait()
    o_step = min(512, s_width)
    out_copies = []
    for g in range(kv_heads):
        for p in range(pieces):
            pass_on(g * pieces + p)
        for p in range(pieces):
            gathered(g * pieces + p)
        part = ctx[:, g * wide_g : (g + 1) * wide_g]
        for i in range(s_width // o_step):
            at = i * o_step
            value = dot(part, ow[g * wide_g : (g + 1) * wide_g, at : at + o_step])
            if g > 0:
                value = value + oterm[:, at : at + o_step]
            oterm[:, at : at + o_step] = value
            if g < kv_heads - 1:
                continue
            osend[:, at : at + o_step] = value.astype(BF16)
            for j in range(chips):
                out_copies.append(
                    remote(
                        osend.at[block(2 * j + 1 - core, share), pl.ds(at, o_step)],
                        opair.at[j, :, pl.ds(at, o_step)], out_s.at[i, j], out_r.at[i, j], {"tp": partner},
                    )
                )
                go(out_copies[-1])

    far_copies = []
    for i in range(s_width // o_step):
        cols = slice(i * o_step, (i + 1) * o_step)
        for copy in out_copies[i * chips : (i + 1) * chips]:
            copy.wait_recv()
        for e in range(1, chips):
            to = lax.rem(chip + e, chips)
            there = block(2 * to + core, share)
            osum[e - 1, :, cols] = (oterm[there, cols] + opair[to, :, cols].astype(F32)).astype(BF16)
            far_copies.append(
                remote(
                    osum.at[e - 1, :, pl.ds(i * o_step, o_step)], ors.at[e - 1, :, pl.ds(i * o_step, o_step)],
                    far_s.at[i, e - 1], far_r.at[i, e - 1], {"tp": 2 * to + core},
                )
            )
            go(far_copies[-1])

    out_rows = block(t, share)
    for i in range(s_width // o_step):
        cols = slice(i * o_step, (i + 1) * o_step)
        oown[:, cols] = (
            xin[out_rows, cols].astype(F32) + (oterm[out_rows, cols] + opair[chip, :, cols].astype(F32))
        )
    for i in range(s_width // o_step):
        cols = slice(i * o_step, (i + 1) * o_step)
        for copy in far_copies[i * (chips - 1) : (i + 1) * (chips - 1)]:
            copy.wait_recv()
        value = oown[:, cols]
        for e in range(1, chips):
            value = value + ors[e - 1, :, cols].astype(F32)
        out[:, cols] = value.astype(BF16)

    for copy in sends:
        copy.wait_send()
    for index in range(len(chunks)):
        for k in range(n - 1):
            chunk_copy(index, k).wait_send()
    for index in range(kv_heads * pieces):
        when(jnp.logical_not(is_end) if relays else True, lambda: ctx_copy(index, 0).wait_send())
        for k in range(1, n - 1):
            ctx_copy(index, k).wait_send()
        when(is_next if relays else False, lambda: pass_copy(index).wait_send())


def on_device(
    n, n_tp, hidden, input_norm_gain, request_adapter, cache_fill_length, query_weight, key_weight,
    value_weight, output_weight, down_weight_all, query_up_weight, value_up_weight,
    rotated_key_cache, stored_value_cache,
):
    rows, model = hidden.shape
    q_width, kv_width = query_weight.shape[1], key_weight.shape[1]
    s_width, t_width = query_weight.shape[0], down_weight_all.shape[0]
    ranks2 = down_weight_all.shape[1]
    cap = max(2, (2 * rows + n - 1) // n)
    cap = (cap + 15) // 16 * 16
    share = n * rows // n_tp
    chips = n_tp // 2
    total = q_width + 2 * kv_width
    kv_heads, heads = kv_width // HEAD_WIDTH, q_width // HEAD_WIDTH
    halfway = HEAD_WIDTH // 2
    frequency = np.float32(ROPE_BASE) ** (np.float32(-2.0) * np.arange(halfway, dtype=np.float32) / np.float32(HEAD_WIDTH))
    frequency = jnp.asarray(np.concatenate([frequency, frequency])[None, :])
    big = [query_weight, key_weight, value_weight, output_weight, down_weight_all, query_up_weight,
           value_up_weight, rotated_key_cache, stored_value_cache]
    chunks = 1 + q_width // min(512, GROUPS * HEAD_WIDTH)
    o_chunks = s_width // min(512, s_width)
    pieces = rows // min(16, rows)
    per_pack = ranks2 // (2 * ADAPTER_RANK)
    packs = (n + per_pack - 1) // per_pack
    vmem = pl.BlockSpec(memory_space=pltpu.VMEM)
    dma = pltpu.SemaphoreType.DMA
    v = pltpu.VMEM
    lanes = 128
    scratch = [v(hidden.shape, hidden.dtype)] + [v(w.shape, w.dtype) for w in big] + [
        v((model // lanes, lanes), BF16), v((1, rows), jnp.int32), v((1, rows), jnp.int32), v((1, lanes), F32),
        pltpu.SMEM((1, rows), jnp.int32),
        v((model // lanes, lanes), F32),
        v((rows, model), BF16),
        v((n, 8, lanes), F32),
        v((n, cap, t_width), BF16),
        v((n, cap, t_width), BF16),
        v((n * rows, s_width), BF16),
        v((n * rows, s_width), BF16),
        v((packs * cap, ranks2), F32),
        v((n_tp - 1, packs * cap, ranks2), F32),
        v((n * rows, total), BF16),
        v((n * rows, total), F32),
        v((n + 1, rows, total), BF16),
        v((rows, heads, HEAD_WIDTH), F32),
        v((rows, kv_heads, HEAD_WIDTH), F32),
        v((rows, kv_heads, HEAD_WIDTH), F32),
        v((rows, heads, HEAD_WIDTH), F32),
        v((n * rows, q_width), BF16),
        v((n * rows, s_width), BF16),
        v((n * rows, s_width), F32),
        v((chips, share, s_width), BF16),
        v((chips - 1, share, s_width), BF16),
        v((share, s_width), F32),
        v((chips - 1, share, s_width), BF16),
        dma, dma((5,)), dma((9,)),
        dma((n - 1,)), dma((n,)),
        dma((n - 1,)), dma((n,)),
        dma((n - 1,)), dma((n,)),
        dma((n,)), dma((n,)),
        dma((n_tp - 1,)), dma((n_tp - 1,)),
        dma((chunks, n - 1)), dma((chunks, n + 1)),
        dma((kv_heads * pieces, n)), dma((kv_heads * pieces, n)),
        dma((o_chunks, chips)), dma((o_chunks, chips)),
        dma((o_chunks, chips - 1)), dma((o_chunks, chips - 1)),
    ]
    shapes = [((share, s_width), BF16), ((rows, kv_width), BF16), ((rows, kv_width), BF16)]
    held = pl.pallas_call(
        functools.partial(kernel, n, n_tp),
        out_shape=[pltpu.VMEM(*one) for one in shapes],
        in_specs=[pl.BlockSpec(memory_space=pl.ANY)] * 14,
        out_specs=[vmem] * 3,
        scratch_shapes=scratch,
        compiler_params=pltpu.CompilerParams(
            collective_id=0, has_side_effects=True, vmem_limit_bytes=62 * 1024 * 1024
        ),
    )(
        hidden, input_norm_gain.reshape(model // lanes, lanes), request_adapter[None, :],
        cache_fill_length[None, :], frequency, *big,
    )
    return tuple(held)


def solution(mesh):
    return jax.shard_map(
        functools.partial(on_device, mesh.shape["ada"], mesh.shape["tp"]),
        mesh=mesh,
        in_specs=(
            P(("rep", "ada"), None),
            P(),
            P(("rep", "ada")),
            P(("rep", "ada")),
            P("ada", "tp"),
            P("ada", "tp"),
            P("ada", "tp"),
            P("tp", "ada"),
            P("tp", "ada"),
            P("ada", "tp"),
            P("ada", "tp"),
            P(("rep", "ada"), None, "tp"),
            P(("rep", "ada"), None, "tp"),
        ),
        out_specs=(P(("rep", "tp"), "ada"), P(("rep", "ada"), "tp"), P(("rep", "ada"), "tp")),
        check_vma=False,
    )
```

time: 60 us -> 53.8 us (0.90)
  Pallas kernels: 57.2 us -> 51 us
    pallas_call x1, Pallas kernels: 57.2 us -> 51 us  [on_device(): pl.pallas_call(functools.partial(kernel, n, n_tp), out_shape=[pltpu.VMEM(...]
where the time goes in v2:
time: 53.8 us; the launch traced here: 53.5 us
  Pallas kernels  51 us (95%)
  local copies, waits for them, and re-layouts  1.87 us (3%)
  between operations  0.64 us (1%)
    pallas_call x1, Pallas kernels, on_device(): pl.pallas_call(functools.partial(kernel, n, n_tp), out_shape=[pltpu.VMEM(...  51 us
    unnamed x3, local copies, waits for them, and re-layouts  1.87 us

profile of v2, /device:TPU:0, one launch (start us, length us, event | category | flops | bytes accessed | tf_op | source)
XLA Modules:
  0.0 53.5 jit_solution(16647201686946693093)
XLA Ops:
  0.6 51.0 %shard_map.157 = (bf16[32,2048]{1,0:T(8,128)(2,1)S(1)}, bf16[32,256]{1,0:T(8,128)(2,1)S(1)}, bf16[32,256]{1,0:T(8,128)(2,1)S(1)}) custom-call(bf16[32,8192]{1,0:T(8,128)(2,1)} %hid_h.1, bf16[64,128]{1,0:T(8,128)(2,1)} %bitcast.3, s32[1,32]{1,0:T(1,128)} %bitcast.4, s32[1,32]{1,0:T(1,128)} %bitcast.5, f32[1,128]{1,0:T(1,128)} %constant.2.clone.freq_h, ...), custom_call_target="tpu_custom_call" | custom-call | tf_op jit(solution)/shard_map/pallas_call | solution.py:598
  51.7 0.7 %copy.20 = bf16[32,2048]{1,0:T(8,128)(2,1)} copy(bf16[32,2048]{1,0:T(8,128)(2,1)S(1)} %get-tuple-element.3) | data formatting | bytes 262144
  52.3 0.6 %copy.21 = bf16[32,256]{1,0:T(8,128)(2,1)} copy(bf16[32,256]{1,0:T(8,128)(2,1)S(1)} %get-tuple-element.4) | data formatting | bytes 32768
  52.9 0.6 %copy.22 = bf16[32,256]{1,0:T(8,128)(2,1)} copy(bf16[32,256]{1,0:T(8,128)(2,1)S(1)} %get-tuple-element.5) | data formatting | bytes 32768

commit v3 on v2

--- a/solution.py
+++ b/solution.py
@@ -19,7 +19,7 @@
 F32 = jnp.float32
 BF16 = jnp.bfloat16
 GROUPS = QUERY_HEAD_COUNT // KEY_VALUE_HEADS
-REQ_STEP = 8
+REQ_STEP = 16
 
 
 def dot(a, b):
@@ -36,11 +36,10 @@
     n, n_tp,
     hid_h, gain_h, ids_h, fill_h, freq_h, qw_h, kw_h, vw_h, ow_h, dw_h, qu_h, vu_h, kc_h, vc_h,
     out, nk_out, nv_out,
-    hid, qw, kw, vw, ow, dw, qu, vu, kc, vc,
+    hid, qw, kvw, ow, dw, qu, vu, kvc,
     gain, ids_row, fill_row, freq, fill, wide_gain, normed, meta, route, rin, xin, xnorm, shr, shr_in, tsend, term, rs, rq3, nk3, nv3, ctx3, ctx,
     osend, oterm, opair, osum, oown, ors,
-    hid_sem, small_sem, load_sem, meta_s, meta_r, route_s, route_r, x_s, x_r, pair_s, pair_r, shr_s, shr_r, rs_s, rs_r,
-    ctx_s, ctx_r, out_s, out_r, far_s, far_r,
+    small_sem, load_sem, send_sem, one_r, x_r, rs_r, ctx_r, out_r, far_r,
 ):
     a = lax.axis_index("ada")
     t = lax.axis_index("tp")
@@ -51,9 +50,12 @@
     t_width, ranks2 = dw.shape
     s_width = xin.shape[1]
     half = s_width // 2
-    q_width, kv_width = qw.shape[1], kw.shape[1]
+    q_width, kv_width = qw.shape[1], kvw.shape[2]
     kv_heads = kv_width // HEAD_WIDTH
-    share = oown.shape[0]
+    pieces, _, piece, _ = ctx.shape
+    sub = oown.shape[1]
+    meta_s, route_s, x_s, pair_s, shr_s, rs_s, ctx_s, out_s, far_s = [send_sem.at[i] for i in range(9)]
+    meta_r, route_r, pair_r, shr_r = [one_r.at[i] for i in range(4)]
     chips = n_tp // 2
     chip = t // 2
     pair = 2 * ADAPTER_RANK
@@ -83,7 +85,7 @@
         elif condition is not False:
             pl.when(condition)(action)
 
-    hid_load = pltpu.make_async_copy(hid_h, hid, hid_sem)
+    hid_load = pltpu.make_async_copy(hid_h, hid, load_sem.at[9])
     hid_load.start()
     small_loads = [
         pltpu.make_async_copy(src, dst, small_sem.at[i])
@@ -101,7 +103,10 @@
     loads = [
         pltpu.make_async_copy(src, dst, load_sem.at[i])
         for i, (src, dst) in enumerate(
-            [(dw_h, dw), (qu_h, qu), (vu_h, vu), (kw_h, kw), (vw_h, vw), (qw_h, qw), (kc_h, kc), (vc_h, vc), (ow_h, ow)]
+            [
+                (dw_h, dw), (qu_h, qu), (vu_h, vu), (kw_h, kvw.at[0]), (vw_h, kvw.at[1]), (qw_h, qw),
+                (kc_h, kvc.at[0]), (vc_h, kvc.at[1]), (ow_h, ow),
+            ]
         )
     ]
     for load in loads:
@@ -137,7 +142,7 @@
     if relays:
         @pl.when(is_end)
         def _():
-            rs[peer(0), :, :q_width] = jnp.zeros((rows, q_width), rs.dtype)
+            rs[peer(0)] = jnp.zeros(rs.shape[1:], rs.dtype)
 
     hid_load.wait()
     squares = jnp.zeros((rows, step), F32)
@@ -158,33 +163,29 @@
     xin[my_rows, :] = hid[:, block(a, s_width)]
 
     pl.semaphore_wait(barrier, n - 1 + n_tp - 1)
-    sends = []
-
-    def go(copy):
-        copy.start()
-        sends.append(copy)
-
     for k in range(n - 1):
         to = peer(k)
-        go(remote(meta.at[a], meta.at[a], meta_s.at[k], meta_r.at[a], {"ada": to}))
+        remote(meta.at[a], meta.at[a], meta_s, meta_r, {"ada": to}).start()
     for k in range(n - 1):
         to = peer(k)
-        go(remote(route.at[to], rin.at[a], route_s.at[k], route_r.at[a], {"ada": to}))
-    for k in range(n - 1):
+        remote(route.at[to], rin.at[a], route_s, route_r, {"ada": to}).start()
+    for k in reversed(range(n - 1)):
         to = peer(k)
-        go(
-            remote(
-                hid.at[:, pl.ds(pl.multiple_of(to * s_width + core * half, 128), half)],
-                xin.at[my_rows, my_half], x_s.at[k], x_r.at[a], {"ada": to},
-            )
-        )
+        remote(
+            hid.at[:, pl.ds(pl.multiple_of(to * s_width + core * half, 128), half)],
+            xin.at[my_rows, my_half], x_s, x_r.at[a], {"ada": to},
+        ).start()
     near_first = [peer(k) for k in reversed(range(n - 1))]
 
     def landed(dst, send, recv):
         remote(dst, dst, send, recv, {"ada": lax.rem(a + 1, n)}).wait_recv()
 
-    for s in near_first:
-        landed(meta.at[s], meta_s.at[0], meta_r.at[s])
+    def sent(src, send):
+        remote(src, src, send, meta_r, {"ada": lax.rem(a + 1, n)}).wait_send()
+
+    others = pl.ds(0, n - 1)
+    other_rows = pl.ds(0, (n - 1) * rows)
+    landed(meta.at[others], meta_s, meta_r)
     lane_cap = lax.broadcasted_iota(jnp.int32, (cap, ranks2), 1) // pair
     lane_rows = lax.broadcasted_iota(jnp.int32, (rows, ranks2), 1) // pair
     low_id = (a * held).astype(F32)
@@ -207,8 +208,7 @@
     row_ids = jnp.concatenate(id_cols, axis=0)
 
     loads[0].wait()
-    for s in near_first:
-        landed(rin.at[s], route_s.at[0], route_r.at[s])
+    landed(rin.at[others], route_s, route_r)
     partial = dot(rin[...].reshape(n * cap, t_width), dw[...])
     for first_s in range(0, n, held):
         tile = jnp.zeros((cap, ranks2), F32)
@@ -221,17 +221,16 @@
         shr[first_s // held * cap : (first_s // held + 1) * cap, :] = tile
     for d in range(1, n_tp):
         to = lax.rem(t + d, n_tp)
-        go(remote(shr, shr_in.at[d - 1], shr_s.at[d - 1], shr_r.at[d - 1], {"tp": to}))
+        remote(shr, shr_in.at[d - 1], shr_s, shr_r, {"tp": to}).start()
 
     def x_region(s):
         return xin.at[block(s, rows), my_half]
 
     for s in near_first:
-        landed(x_region(s), x_s.at[0], x_r.at[s])
-        go(remote(x_region(s), x_region(s), pair_s.at[s], pair_r.at[s], {"tp": partner}))
-
-    for copy in sends[-(n - 1) - (n_tp - 1) : -(n - 1)]:
-        copy.wait_recv()
+        landed(x_region(s), x_s, x_r.at[s])
+        remote(x_region(s), x_region(s), pair_s, pair_r, {"tp": partner}).start()
+
+    landed(shr_in, shr_s, shr_r)
     total = shr[...]
     for d in range(1, n_tp):
         total = total + shr_in[d - 1]
@@ -250,9 +249,7 @@
         moved = dot(spread, jnp.where(from_lane == to_lane + offset, 1.0, 0.0).astype(BF16))
         ups.append(jnp.where(own_lane, moved, 0.0).astype(BF16))
 
-    for s in near_first:
-        other = xin.at[block(s, rows), block(1 - core, half)]
-        landed(other, pair_s.at[s], pair_r.at[s])
+    landed(xin.at[other_rows, my_half], pair_s, pair_r)
     for s in range(n):
         rows_s = slice(s * rows, (s + 1) * rows)
         for c in range(0, s_width, step):
@@ -266,15 +263,20 @@
     far_target = peer(0) + end * (beside - peer(0))
     far_slot = a + end * (spare - a)
     chunks = []
+    groups = 1 + kv_heads
+
+    def of_group(index):
+        return 0 if index == 0 else 1 + (index - 1) // per_g
 
     def chunk_copy(index, k):
         at, width = chunks[index]
         cols = pl.ds(at, width)
         to = peer(k)
-        target, slot = (far_target, far_slot) if k == 0 and index > 0 else (to, a)
+        target, slot, mark_at = to, a, of_group(index)
+        if k == 0:
+            target, slot, mark_at = far_target, far_slot, mark_at + end * (groups + index - mark_at)
         return remote(
-            tsend.at[block(to, rows), cols], rs.at[slot, :, cols], rs_s.at[index, k], rs_r.at[index, slot],
-            {"ada": target},
+            tsend.at[block(to, rows), cols], rs.at[slot, :, cols], rs_s, rs_r.at[mark_at], {"ada": target}
         )
 
     def give(value, at, width):
@@ -284,7 +286,7 @@
         tsend[:, at : at + width] = value.astype(BF16)
 
     def ship(index, k):
-        direct = k > 0 or index == 0 or not relays
+        direct = k > 0 or not relays
         when(True if direct else jnp.logical_not(is_next), lambda: chunk_copy(index, k).start())
 
     def relay(index):
@@ -295,32 +297,33 @@
 
         @pl.when(is_next)
         def _():
-            landed(rs.at[spare, :, cols], rs_s.at[index, 0], rs_r.at[index, spare])
+            landed(rs.at[spare, :, cols], rs_s, rs_r.at[groups + index])
             there = block(peer(0), rows)
             tsend[there, cols] = (term[there, cols] + rs[spare, :, cols].astype(F32)).astype(BF16)
             remote(
-                tsend.at[there, cols], rs.at[a, :, cols], rs_s.at[index, 0], rs_r.at[index, a], {"ada": peer(0)}
+                tsend.at[there, cols], rs.at[a, :, cols], rs_s, rs_r.at[of_group(index)], {"ada": peer(0)}
             ).start()
 
-    def arrived(index):
-        at, width = chunks[index]
-        cols = pl.ds(at, width)
-        for k in reversed(range(n - 1)):
-            s = peer(k)
-            when(
-                jnp.logical_not(is_end) if relays and k == 0 and index > 0 else True,
-                lambda: landed(rs.at[s, :, cols], rs_s.at[index, 0], rs_r.at[index, s]),
-            )
-
-    x = xnorm[...]
-    give(
-        jnp.concatenate([dot(x, kw[...]), dot(x, vw[...]) + dot(ups[1], vu[...])], axis=1), q_width, 2 * kv_width
-    )
-    for k in range(n - 1):
-        ship(0, k)
+    def arrived(group):
+        cols = pl.ds(q_width, 2 * kv_width) if group == 0 else pl.ds((group - 1) * wide_g, wide_g)
+
+        def take(count):
+            landed(rs.at[pl.ds(0, count), :, cols], rs_s, rs_r.at[group])
+
+        if not relays:
+            take(n - 1)
+        else:
+            pl.when(is_end)(lambda: take(n - 2))
+            pl.when(jnp.logical_not(is_end))(lambda: take(n - 1))
+
     wide_g = GROUPS * HEAD_WIDTH
     q_step = min(512, wide_g)
     per_g = wide_g // q_step
+    x = xnorm[...]
+    give(
+        jnp.concatenate([dot(x, kvw[0]), dot(x, kvw[1]) + dot(ups[1], vu[...])], axis=1), q_width, 2 * kv_width
+    )
+    ship(0, 0)
     for g in range(kv_heads):
         group = range(1 + g * per_g, 1 + (g + 1) * per_g)
         for index in group:
@@ -330,9 +333,9 @@
                 ship(index, 0)
         if g == 0:
             for k in range(1, n - 1):
-                for index in group:
+                for index in [0, *group]:
                     ship(index, k)
-    for index in range(1, 1 + per_g):
+    for index in range(1 + per_g):
         relay(index)
     for g in range(1, kv_heads):
         for k in range(n - 1):
@@ -366,7 +369,7 @@
         for j in range(REQ_STEP):
             r = start + j
             q = rq3[r, g * GROUPS : (g + 1) * GROUPS, :]
-            keys = kc[r, :, g * HEAD_WIDTH : (g + 1) * HEAD_WIDTH]
+            keys = kvc[0, r, :, g * HEAD_WIDTH : (g + 1) * HEAD_WIDTH]
             score_list.append(
                 lax.dot_general(q.astype(BF16), keys, (((1,), (1,)), ((), ())), preferred_element_type=F32)
             )
@@ -386,31 +389,21 @@
         own_part = (own_exp * scale).astype(BF16).astype(F32) * jnp.concatenate(val_list, axis=0)
         for j in range(REQ_STEP):
             r = start + j
-            values = vc[r, :, g * HEAD_WIDTH : (g + 1) * HEAD_WIDTH]
+            values = kvc[1, r, :, g * HEAD_WIDTH : (g + 1) * HEAD_WIDTH]
             b = slice(j * GROUPS, (j + 1) * GROUPS)
             ctx3[r, g * GROUPS : (g + 1) * GROUPS, :] = dot(low[b], values) + own_part[b]
 
-    piece = min(16, rows)
-    pieces = rows // piece
-
     def ctx_region(s, index):
-        g, p = index // pieces, index % pieces
-        return ctx.at[pl.ds(pl.multiple_of(s * rows + p * piece, piece), piece), pl.ds(g * wide_g, wide_g)]
-
-    def ctx_copy(index, k):
-        return remote(
-            ctx_region(a, index), ctx_region(a, index), ctx_s.at[index, k], ctx_r.at[index, a], {"ada": peer(k)}
-        )
-
-    def pass_copy(index):
-        s = peer(0)
-        outward = lax.div(a, n - 2) * (n - 1)
-        return remote(
-            ctx_region(s, index), ctx_region(s, index), ctx_s.at[index, n - 1], ctx_r.at[index, s], {"ada": outward}
-        )
-
-    def ctx_landed(s, index):
-        landed(ctx_region(s, index), ctx_s.at[index, 0], ctx_r.at[index, s])
+        return ctx.at[index % pieces, s, :, pl.ds(index // pieces * wide_g, wide_g)]
+
+    def ctx_send(index):
+        here = ctx_region(a, index)
+        for k in range(1 if relays else 0, n - 1):
+            copy = remote(here, here, ctx_s, ctx_r.at[index, a], {"ada": peer(k)})
+            when(jnp.logical_or(is_end, is_next) if relays and k == n - 2 else True, copy.start)
+
+    def ctx_landed(index, k):
+        landed(ctx_region(peer(k), index), ctx_s, ctx_r.at[index, peer(k)])
 
     def pass_on(index):
         if not relays:
@@ -418,21 +411,20 @@
 
         @pl.when(is_next)
         def _():
-            ctx_landed(peer(0), index)
-            pass_copy(index).start()
+            for k in reversed(range(n - 2)):
+                there = ctx_region(peer(k), index)
+                ctx_landed(index, k)
+                remote(
+                    there, there, ctx_s, ctx_r.at[index, peer(k)], {"ada": lax.div(a, n - 2) * (n - 1)}
+                ).start()
 
     def gathered(index):
         for k in reversed(range(n - 1)):
-            s = peer(k)
-            when(
-                jnp.logical_not(is_next) if relays and k == 0 else True,
-                lambda: ctx_landed(s, index),
-            )
+            when(jnp.logical_not(is_next) if relays and k < n - 2 else True, lambda: ctx_landed(index, k))
 
     turned = 0
     for g in range(kv_heads):
-        for index in range(1 + g * per_g, 1 + (g + 1) * per_g):
-            arrived(index)
+        arrived(1 + g)
         while turned < (g + 1) * GROUPS:
             rq3[:, turned, :] = turn(summed(turned * HEAD_WIDTH, HEAD_WIDTH)).astype(F32)
             turned += 1
@@ -447,85 +439,117 @@
             def _(i):
                 attend(g, p * piece + i * REQ_STEP)
 
-            own_rows = pl.ds(pl.multiple_of(a * rows + p * piece, piece), piece)
             for h in range(g * GROUPS, (g + 1) * GROUPS):
-                ctx[own_rows, h * HEAD_WIDTH : (h + 1) * HEAD_WIDTH] = ctx3[
+                ctx[p, a, :, h * HEAD_WIDTH : (h + 1) * HEAD_WIDTH] = ctx3[
                     p * piece : (p + 1) * piece, h, :
                 ].astype(BF16)
             index = g * pieces + p
-            when(jnp.logical_not(is_end) if relays else True, lambda: ctx_copy(index, 0).start())
-            for k in range(1, n - 1):
-                ctx_copy(index, k).start()
+            ctx_send(index)
 
     loads[8].wait()
-    o_step = min(512, s_width)
-    out_copies = []
-    for g in range(kv_heads):
+    o_step = min(1024, s_width)
+    o_chunks = s_width // o_step
+    span = n * piece
+
+    def to_partner(p, i):
+        cols = pl.ds(i * o_step, o_step)
+        for j in range(chips):
+            mine = pl.ds(pl.multiple_of(p * span + (2 * j + 1 - core) * sub, sub), sub)
+            remote(
+                osend.at[mine, cols], opair.at[p, j, :, cols], out_s, out_r.at[p * o_chunks + i], {"tp": partner}
+            ).start()
+
+    def part_of(p, i, whose):
+        at = slice(i * o_step, (i + 1) * o_step)
+        there = pl.ds(pl.multiple_of(p * span + (2 * whose + core) * sub, sub), sub)
+        return oterm[there, at] + opair[p, whose, :, at].astype(F32)
+
+    def to_chips(p):
+        for i in range(o_chunks):
+            cols = pl.ds(i * o_step, o_step)
+            landed(opair.at[p, :, :, cols], out_s, out_r.at[p * o_chunks + i])
+            for e in range(1, chips):
+                to = lax.rem(chip + e, chips)
+                osum[p, e - 1, :, i * o_step : (i + 1) * o_step] = part_of(p, i, to).astype(BF16)
+                remote(
+                    osum.at[p, e - 1, :, cols], ors.at[p, e - 1, :, cols], far_s, far_r.at[p * o_chunks + i],
+                    {"tp": 2 * to + core},
+                ).start()
+
+    for g in range(kv_heads - 1):
         for p in range(pieces):
             pass_on(g * pieces + p)
         for p in range(pieces):
             gathered(g * pieces + p)
-        part = ctx[:, g * wide_g : (g + 1) * wide_g]
-        for i in range(s_width // o_step):
+        part = ctx[:, :, :, g * wide_g : (g + 1) * wide_g].reshape(pieces * span, wide_g)
+        for at in range(0, s_width, o_step):
+            value = dot(part, ow[g * wide_g : (g + 1) * wide_g, at : at + o_step])
+            oterm[:, at : at + o_step] = value + oterm[:, at : at + o_step] if g > 0 else value
+    g = kv_heads - 1
+    for p in range(pieces):
+        pass_on(g * pieces + p)
+    for p in range(pieces):
+        gathered(g * pieces + p)
+        part = ctx[p, :, :, g * wide_g : (g + 1) * wide_g].reshape(span, wide_g)
+        these = slice(p * span, (p + 1) * span)
+        for i in range(o_chunks):
             at = i * o_step
             value = dot(part, ow[g * wide_g : (g + 1) * wide_g, at : at + o_step])
             if g > 0:
-                value = value + oterm[:, at : at + o_step]
-            oterm[:, at : at + o_step] = value
-            if g < kv_heads - 1:
-                continue
-            osend[:, at : at + o_step] = value.astype(BF16)
-            for j in range(chips):
-                out_copies.append(
-                    remote(
-                        osend.at[block(2 * j + 1 - core, share), pl.ds(at, o_step)],
-                        opair.at[j, :, pl.ds(at, o_step)], out_s.at[i, j], out_r.at[i, j], {"tp": partner},
-                    )
-                )
-                go(out_copies[-1])
-
-    far_copies = []
-    for i in range(s_width // o_step):
-        cols = slice(i * o_step, (i + 1) * o_step)
-        for copy in out_copies[i * chips : (i + 1) * chips]:
-            copy.wait_recv()
-        for e in range(1, chips):
-            to = lax.rem(chip + e, chips)
-            there = block(2 * to + core, share)
-            osum[e - 1, :, cols] = (oterm[there, cols] + opair[to, :, cols].astype(F32)).astype(BF16)
-            far_copies.append(
-                remote(
-                    osum.at[e - 1, :, pl.ds(i * o_step, o_step)], ors.at[e - 1, :, pl.ds(i * o_step, o_step)],
-                    far_s.at[i, e - 1], far_r.at[i, e - 1], {"tp": 2 * to + core},
-                )
+                value = value + oterm[these, at : at + o_step]
+            oterm[these, at : at + o_step] = value
+            osend[these, at : at + o_step] = value.astype(BF16)
+            to_partner(p, i)
+    for p in range(pieces):
+        to_chips(p)
+
+    homes = sub // piece
+    for p in range(pieces):
+        for i in range(o_chunks):
+            cols = slice(i * o_step, (i + 1) * o_step)
+            residual = jnp.concatenate(
+                [
+                    xin[pl.ds(pl.multiple_of((t * homes + h) * rows + p * piece, piece), piece), cols]
+                    for h in range(homes)
+                ],
+                axis=0,
             )
-            go(far_copies[-1])
-
-    out_rows = block(t, share)
-    for i in range(s_width // o_step):
-        cols = slice(i * o_step, (i + 1) * o_step)
-        oown[:, cols] = (
-            xin[out_rows, cols].astype(F32) + (oterm[out_rows, cols] + opair[chip, :, cols].astype(F32))
-        )
-    for i in range(s_width // o_step):
-        cols = slice(i * o_step, (i + 1) * o_step)
-        for copy in far_copies[i * (chips - 1) : (i + 1) * (chips - 1)]:
-            copy.wait_recv()
-        value = oown[:, cols]
-        for e in range(1, chips):
-            value = value + ors[e - 1, :, cols].astype(F32)
-        out[:, cols] = value.astype(BF16)
-
-    for copy in sends:
-        copy.wait_send()
-    for index in range(len(chunks)):
-        for k in range(n - 1):
-            chunk_copy(index, k).wait_send()
-    for index in range(kv_heads * pieces):
-        when(jnp.logical_not(is_end) if relays else True, lambda: ctx_copy(index, 0).wait_send())
-        for k in range(1, n - 1):
-            ctx_copy(index, k).wait_send()
-        when(is_next if relays else False, lambda: pass_copy(index).wait_send())
+            oown[p, :, cols] = residual.astype(F32) + part_of(p, i, chip)
+    for p in range(pieces):
+        for i in range(o_chunks):
+            cols = slice(i * o_step, (i + 1) * o_step)
+            landed(ors.at[p, :, :, pl.ds(i * o_step, o_step)], far_s, far_r.at[p * o_chunks + i])
+            value = oown[p, :, cols]
+            for e in range(1, chips):
+                value = value + ors[p, e - 1, :, cols].astype(F32)
+            for h in range(homes):
+                out[h * rows + p * piece : h * rows + (p + 1) * piece, cols] = value[
+                    h * piece : (h + 1) * piece
+                ].astype(BF16)
+
+    sent(meta.at[others], meta_s)
+    sent(route.at[others], route_s)
+    sent(xin.at[other_rows, my_half], x_s)
+    sent(xin.at[other_rows, my_half], pair_s)
+    sent(shr_in, shr_s)
+    sent(tsend.at[other_rows], rs_s)
+    if relays:
+        sent(ctx.at[:, pl.ds(0, n - 3)], ctx_s)
+        pl.when(jnp.logical_or(is_end, is_next))(lambda: sent(ctx.at[:, pl.ds(0, 1)], ctx_s))
+        pl.when(is_next)(lambda: sent(ctx.at[:, pl.ds(0, n - 2)], ctx_s))
+    else:
+        sent(ctx.at[:, others], ctx_s)
+    sent(osend.at[pl.ds(0, pieces * chips * sub)], out_s)
+    sent(osum, far_s)
+
+
+def put_out(*refs):
+    sems = refs[6]
+    copies = [pltpu.make_async_copy(refs[i], refs[3 + i], sems.at[i]) for i in range(3)]
+    for copy in copies:
+        copy.start()
+    for copy in copies:
+        copy.wait()
 
 
 def on_device(
@@ -549,15 +573,19 @@
     big = [query_weight, key_weight, value_weight, output_weight, down_weight_all, query_up_weight,
            value_up_weight, rotated_key_cache, stored_value_cache]
     chunks = 1 + q_width // min(512, GROUPS * HEAD_WIDTH)
-    o_chunks = s_width // min(512, s_width)
-    pieces = rows // min(16, rows)
+    o_chunks = s_width // min(1024, s_width)
+    piece = min(16, rows)
+    pieces = rows // piece
     per_pack = ranks2 // (2 * ADAPTER_RANK)
     packs = (n + per_pack - 1) // per_pack
     vmem = pl.BlockSpec(memory_space=pltpu.VMEM)
     dma = pltpu.SemaphoreType.DMA
     v = pltpu.VMEM
     lanes = 128
-    scratch = [v(hidden.shape, hidden.dtype)] + [v(w.shape, w.dtype) for w in big] + [
+    scratch = [v(hidden.shape, hidden.dtype)] + [
+        v(query_weight.shape, BF16), v((2, *key_weight.shape), BF16), v(output_weight.shape, BF16),
+        v(down_weight_all.shape, BF16), v(query_up_weight.shape, BF16), v(value_up_weight.shape, BF16),
+        v((2, *rotated_key_cache.shape), BF16),
         v((model // lanes, lanes), BF16), v((1, rows), jnp.int32), v((1, rows), jnp.int32), v((1, lanes), F32),
         pltpu.SMEM((1, rows), jnp.int32),
         v((model // lanes, lanes), F32),
@@ -576,23 +604,16 @@
         v((rows, kv_heads, HEAD_WIDTH), F32),
         v((rows, kv_heads, HEAD_WIDTH), F32),
         v((rows, heads, HEAD_WIDTH), F32),
-        v((n * rows, q_width), BF16),
+        v((pieces, n, piece, q_width), BF16),
         v((n * rows, s_width), BF16),
         v((n * rows, s_width), F32),
-        v((chips, share, s_width), BF16),
-        v((chips - 1, share, s_width), BF16),
-        v((share, s_width), F32),
-        v((chips - 1, share, s_width), BF16),
-        dma, dma((5,)), dma((9,)),
-        dma((n - 1,)), dma((n,)),
-        dma((n - 1,)), dma((n,)),
-        dma((n - 1,)), dma((n,)),
-        dma((n,)), dma((n,)),
-        dma((n_tp - 1,)), dma((n_tp - 1,)),
-        dma((chunks, n - 1)), dma((chunks, n + 1)),
-        dma((kv_heads * pieces, n)), dma((kv_heads * pieces, n)),
-        dma((o_chunks, chips)), dma((o_chunks, chips)),
-        dma((o_chunks, chips - 1)), dma((o_chunks, chips - 1)),
+        v((pieces, chips, share // pieces, s_width), BF16),
+        v((pieces, chips - 1, share // pieces, s_width), BF16),
+        v((pieces, share // pieces, s_width), F32),
+        v((pieces, chips - 1, share // pieces, s_width), BF16),
+        dma((5,)), dma((10,)), dma((9,)), dma((4,)), dma((n,)),
+        dma((1 + kv_heads + chunks,)), dma((kv_heads * pieces, n)), dma((pieces * o_chunks,)),
+        dma((pieces * o_chunks,)),
     ]
     shapes = [((share, s_width), BF16), ((rows, kv_width), BF16), ((rows, kv_width), BF16)]
     held = pl.pallas_call(
@@ -608,7 +629,16 @@
         hidden, input_norm_gain.reshape(model // lanes, lanes), request_adapter[None, :],
         cache_fill_length[None, :], frequency, *big,
     )
-    return tuple(held)
+    held = [pltpu.with_memory_space_constraint(one, pltpu.VMEM) for one in held]
+    return tuple(
+        pl.pallas_call(
+            put_out,
+            out_shape=[jax.ShapeDtypeStruct(*one) for one in shapes],
+            in_specs=[vmem] * 3,
+            out_specs=[pl.BlockSpec(memory_space=pl.ANY)] * 3,
+            scratch_shapes=[dma((3,))],
+        )(*held)
+    )
 
 
 def solution(mesh):

time: 53.8 us -> 50.7 us (0.942)
  local copies, waits for them, and re-layouts: 1.87 us -> 0 us
  Pallas kernels: 51 us -> 49.8 us
    pallas_call x1, Pallas kernels: 51 us -> 49.2 us  [on_device(): pl.pallas_call(functools.partial(kernel, n, n_tp), out_shape=[pltpu.VMEM(...]
    unnamed x3 -> x0, local copies, waits for them, and re-layouts: 1.87 us -> none
    pallas_call x0 -> x1, Pallas kernels: none -> 0.69 us  [on_device(): pl.pallas_call(put_out, out_shape=[jax.ShapeDtypeStruct(*one) for one in...]
where the time goes in v3:
time: 50.7 us; the launch traced here: 50.5 us
  Pallas kernels  49.8 us (98%)
  between operations  0.64 us (1%)
    pallas_call x1, Pallas kernels, on_device(): pl.pallas_call(functools.partial(kernel, n, n_tp), out_shape=[pltpu.VMEM(...  49.2 us

profile of v3, /device:TPU:0, one launch (start us, length us, event | category | flops | bytes accessed | tf_op | source)
XLA Modules:
  0.0 50.5 jit_solution(6533476556378298148)
XLA Ops:
  0.6 49.2 %shard_map.157 = (bf16[32,2048]{1,0:T(8,128)(2,1)S(1)}, bf16[32,256]{1,0:T(8,128)(2,1)S(1)}, bf16[32,256]{1,0:T(8,128)(2,1)S(1)}) custom-call(bf16[32,8192]{1,0:T(8,128)(2,1)} %hid_h.1, bf16[64,128]{1,0:T(8,128)(2,1)} %bitcast.3, s32[1,32]{1,0:T(1,128)} %bitcast.4, s32[1,32]{1,0:T(1,128)} %bitcast.5, f32[1,128]{1,0:T(1,128)} %constant.2.clone.freq_h, ...), custom_call_target="tpu_custom_call" | custom-call | tf_op jit(solution)/shard_map/pallas_call | solution.py:619
  49.8 0.7 %shard_map.158 = (bf16[32,2048]{1,0:T(8,128)(2,1)}, bf16[32,256]{1,0:T(8,128)(2,1)}, bf16[32,256]{1,0:T(8,128)(2,1)}) custom-call(bf16[32,2048]{1,0:T(8,128)(2,1)S(1)} %get-tuple-element.6.refs_0_, bf16[32,256]{1,0:T(8,128)(2,1)S(1)} %get-tuple-element.7.refs_1_, bf16[32,256]{1,0:T(8,128)(2,1)S(1)} %get-tuple-element.8.refs_2_), custom_call_target="tpu_custom_call" | custom-call | tf_op jit(solution)/shard_map/pallas_call | solution.py:634

commit v4 on v3

--- a/solution.py
+++ b/solution.py
@@ -166,15 +166,18 @@
     for k in range(n - 1):
         to = peer(k)
         remote(meta.at[a], meta.at[a], meta_s, meta_r, {"ada": to}).start()
-    for k in range(n - 1):
+
+    def send_route(k):
         to = peer(k)
         remote(route.at[to], rin.at[a], route_s, route_r, {"ada": to}).start()
-    for k in reversed(range(n - 1)):
+
+    def send_x(k):
         to = peer(k)
         remote(
             hid.at[:, pl.ds(pl.multiple_of(to * s_width + core * half, 128), half)],
             xin.at[my_rows, my_half], x_s, x_r.at[a], {"ada": to},
         ).start()
+
     near_first = [peer(k) for k in reversed(range(n - 1))]
 
     def landed(dst, send, recv):
@@ -185,6 +188,28 @@
 
     others = pl.ds(0, n - 1)
     other_rows = pl.ds(0, (n - 1) * rows)
+    def outer():
+        send_route(n - 2)
+        send_x(n - 2)
+        for k in range(n - 2):
+            send_route(k)
+        for k in reversed(range(n - 2)):
+            send_x(k)
+
+    def beside_end():
+        send_route(n - 2)
+        for k in range(n - 2):
+            send_route(k)
+        sent(route.at[others], route_s)
+        send_x(n - 2)
+        for k in reversed(range(n - 2)):
+            send_x(k)
+
+    if relays:
+        pl.when(is_next)(beside_end)
+        pl.when(jnp.logical_not(is_next))(outer)
+    else:
+        outer()
     landed(meta.at[others], meta_s, meta_r)
     lane_cap = lax.broadcasted_iota(jnp.int32, (cap, ranks2), 1) // pair
     lane_rows = lax.broadcasted_iota(jnp.int32, (rows, ranks2), 1) // pair
@@ -398,9 +423,9 @@
 
     def ctx_send(index):
         here = ctx_region(a, index)
-        for k in range(1 if relays else 0, n - 1):
+        for k in range(n - 1):
             copy = remote(here, here, ctx_s, ctx_r.at[index, a], {"ada": peer(k)})
-            when(jnp.logical_or(is_end, is_next) if relays and k == n - 2 else True, copy.start)
+            when(jnp.logical_not(is_end) if relays and k == 0 else True, copy.start)
 
     def ctx_landed(index, k):
         landed(ctx_region(peer(k), index), ctx_s, ctx_r.at[index, peer(k)])
@@ -411,16 +436,15 @@
 
         @pl.when(is_next)
         def _():
-            for k in reversed(range(n - 2)):
-                there = ctx_region(peer(k), index)
-                ctx_landed(index, k)
-                remote(
-                    there, there, ctx_s, ctx_r.at[index, peer(k)], {"ada": lax.div(a, n - 2) * (n - 1)}
-                ).start()
+            there = ctx_region(peer(0), index)
+            ctx_landed(index, 0)
+            remote(
+                there, there, ctx_s, ctx_r.at[index, peer(0)], {"ada": lax.div(a, n - 2) * (n - 1)}
+            ).start()
 
     def gathered(index):
         for k in reversed(range(n - 1)):
-            when(jnp.logical_not(is_next) if relays and k < n - 2 else True, lambda: ctx_landed(index, k))
+            when(jnp.logical_not(is_next) if relays and k == 0 else True, lambda: ctx_landed(index, k))
 
     turned = 0
     for g in range(kv_heads):
@@ -500,8 +524,11 @@
             oterm[these, at : at + o_step] = value
             osend[these, at : at + o_step] = value.astype(BF16)
             to_partner(p, i)
-    for p in range(pieces):
-        to_chips(p)
+            if p > 0 and i == 0:
+                pl.when(core == 0)(lambda: to_chips(p - 1))
+        if p > 0:
+            pl.when(core == 1)(lambda: to_chips(p - 1))
+    to_chips(pieces - 1)
 
     homes = sub // piece
     for p in range(pieces):
@@ -528,15 +555,16 @@
                 ].astype(BF16)
 
     sent(meta.at[others], meta_s)
-    sent(route.at[others], route_s)
+    when(jnp.logical_not(is_next) if relays else True, lambda: sent(route.at[others], route_s))
     sent(xin.at[other_rows, my_half], x_s)
     sent(xin.at[other_rows, my_half], pair_s)
     sent(shr_in, shr_s)
     sent(tsend.at[other_rows], rs_s)
     if relays:
-        sent(ctx.at[:, pl.ds(0, n - 3)], ctx_s)
-        pl.when(jnp.logical_or(is_end, is_next))(lambda: sent(ctx.at[:, pl.ds(0, 1)], ctx_s))
-        pl.when(is_next)(lambda: sent(ctx.at[:, pl.ds(0, n - 2)], ctx_s))
+        pl.when(is_end)(lambda: sent(ctx.at[:, pl.ds(0, n - 2)], ctx_s))
+        pl.when(is_next)(lambda: sent(ctx, ctx_s))
+        inner = jnp.logical_not(jnp.logical_or(is_end, is_next))
+        pl.when(inner)(lambda: sent(ctx.at[:, others], ctx_s))
     else:
         sent(ctx.at[:, others], ctx_s)
     sent(osend.at[pl.ds(0, pieces * chips * sub)], out_s)

time: 50.7 us -> 50.7 us (level)
  no operation moved by 1% of the time
where the time goes in v4:
time: 50.7 us; the launch traced here: 50.5 us
  Pallas kernels  49.8 us (98%)
  between operations  0.64 us (1%)
    pallas_call x1, Pallas kernels, on_device(): pl.pallas_call(functools.partial(kernel, n, n_tp), out_shape=[pltpu.VMEM(...  49.1 us

profile of v4, /device:TPU:0, one launch (start us, length us, event | category | flops | bytes accessed | tf_op | source)
XLA Modules:
  0.0 50.5 jit_solution(15777518612402052480)
XLA Ops:
  0.6 49.1 %shard_map.157 = (bf16[32,2048]{1,0:T(8,128)(2,1)S(1)}, bf16[32,256]{1,0:T(8,128)(2,1)S(1)}, bf16[32,256]{1,0:T(8,128)(2,1)S(1)}) custom-call(bf16[32,8192]{1,0:T(8,128)(2,1)} %hid_h.1, bf16[64,128]{1,0:T(8,128)(2,1)} %bitcast.3, s32[1,32]{1,0:T(1,128)} %bitcast.4, s32[1,32]{1,0:T(1,128)} %bitcast.5, f32[1,128]{1,0:T(1,128)} %constant.2.clone.freq_h, ...), custom_call_target="tpu_custom_call" | custom-call | tf_op jit(solution)/shard_map/pallas_call | solution.py:647
  49.8 0.7 %shard_map.158 = (bf16[32,2048]{1,0:T(8,128)(2,1)}, bf16[32,256]{1,0:T(8,128)(2,1)}, bf16[32,256]{1,0:T(8,128)(2,1)}) custom-call(bf16[32,2048]{1,0:T(8,128)(2,1)S(1)} %get-tuple-element.6.refs_0_, bf16[32,256]{1,0:T(8,128)(2,1)S(1)} %get-tuple-element.7.refs_1_, bf16[32,256]{1,0:T(8,128)(2,1)S(1)} %get-tuple-element.8.refs_2_), custom_call_target="tpu_custom_call" | custom-call | tf_op jit(solution)/shard_map/pallas_call | solution.py:662
